TPU v7x, 32 devices: a whole 2x2x4 slice. The times are simulated.
32 devices in a mesh: dp: 16 (over z, y, core), tensor: 2 (over x).
Axes of the slice: x: 2, y: 2, z: 4, core: 2. Of those that a mesh axis runs over, the one named last changes fastest.
Arguments:
- tokens: bfloat16 [16384, 1024], P('dp'), may hold values from -6 to 6
- cotangent: bfloat16 [16384, 1024], P('dp'), may hold values from -6 to 6
- attn_gain: float32 [1024], replicated, may hold values from 0.1 to 1.9
- mlp_gain: float32 [1024], replicated, may hold values from 0.1 to 1.9
- w_qkv: bfloat16 [1024, 3, 1024], P(None, None, 'tensor'), may hold values from -0.1875 to 0.1875
- w_out: bfloat16 [1024, 1024], P('tensor'), may hold values from -0.75 to 0.75
- w_in: bfloat16 [1024, 2, 2624], P(None, None, 'tensor'), may hold values from -0.1875 to 0.1875
- w_down: bfloat16 [2624, 1024], P('tensor'), may hold values from -0.125 to 0.125
- seq_lengths: int32 [16, 4], replicated, may hold values from 1 to 512, as said below
- set_owner: int32 [16], replicated, may hold values from 0 to 15, each once
- arrival: int32 [1024], replicated, may hold values from 0 to 1023, as said below
Outputs:
- output: float32 [16384, 1024], P('dp')
- grad_tokens: float32 [16384, 1024], P('dp')
- grad_attn_gain: float32 [1024], P('dp')
- grad_mlp_gain: float32 [1024], P('dp')
- grad_qkv: float32 [1024, 3, 1024], P('dp', None, 'tensor')
- grad_out: float32 [1024, 1024], P('tensor', 'dp')
- grad_in: float32 [1024, 2, 2624], P('dp', None, 'tensor')
- grad_down: float32 [2624, 1024], P('tensor', 'dp')
Inputs may be any that keep to these rules, and one draw needn't show every extreme that they name: `seq_lengths`: each row holds the lengths of the 4 sequences of one set; they sum to 1024, and exactly one of them is 512. Set b is taken by data group set_owner[b]; each group takes one set. `arrival`: A permutation of the group layout's pieces; piece p belongs to group p // 64. The 64 pieces that stand on one data index go to 16 groups, exactly 4 to each.
All inputs are finite; a program needn't handle non-finite values.
Results may differ from a plain program's by a relative error of at most 0.017.
The roundings to bfloat16 on the way count: a program that leaves them out, or rounds other values in their place, can miss the bound.
Values may be sent and summed in bfloat16 or wider, within the bound.
A program may use at most 256 MiB of HBM per device.

v0:
```python
import jax
import jax.numpy as jnp
from jax import lax
from jax.sharding import PartitionSpec as P


HEAD = 64
EPSILON = 1e-05
THETA_BASE = 160000.0
SCORE_SCALE = 0.125
MASK_FILL = -1000000000.0
ROOT_HALF = 0.7071067811865476
ROOT_TWO_PI_INV = 0.3989422804014327


def low(values):
    return values.astype(jnp.bfloat16)


def wide(values):
    return values.astype(jnp.float32)


def norm_parts(values):
    centred = values - jnp.mean(values, axis=-1, keepdims=True)
    scale = lax.rsqrt(jnp.mean(centred * centred, axis=-1, keepdims=True) + EPSILON)
    return (centred * scale, scale)


def norm_back(unit, scale, grad):
    mean_grad = jnp.mean(grad, axis=-1, keepdims=True)
    mean_along = jnp.mean(grad * unit, axis=-1, keepdims=True)
    return scale * (grad - mean_grad - unit * mean_along)


def rotary(position):
    halves = HEAD // 2
    frequency = THETA_BASE ** (-2.0 * jnp.arange(halves, dtype=jnp.float32) / HEAD)
    angles = position.astype(jnp.float32)[:, None] * frequency[None, :]
    cosine = jnp.concatenate([jnp.cos(angles), jnp.cos(angles)], axis=-1)[:, None, :]
    sine = jnp.concatenate([jnp.sin(angles), jnp.sin(angles)], axis=-1)[:, None, :]
    return (cosine, sine)


def spin(values, cosine, sine):
    halves = values.shape[-1] // 2
    turned = jnp.concatenate([-values[..., halves:], values[..., :halves]], axis=-1)
    return values * cosine + turned * sine


def spin_back(grads, cosine, sine):
    halves = grads.shape[-1] // 2
    scaled = grads * sine
    turned = jnp.concatenate([scaled[..., halves:], -scaled[..., :halves]], axis=-1)
    return grads * cosine + turned


def segments(lengths_row, row_count):
    ends = jnp.cumsum(lengths_row)
    rows = jnp.arange(row_count, dtype=jnp.int32)
    segment = jnp.sum((rows[:, None] >= ends[None, :]).astype(jnp.int32), axis=1)
    starts = ends - lengths_row
    matches = segment[:, None] == jnp.arange(lengths_row.shape[0], dtype=jnp.int32)[None, :]
    first_rows = jnp.sum(jnp.where(matches, starts[None, :], 0), axis=1)
    long_start = jnp.sum(jnp.where(lengths_row * 2 == row_count, starts, 0))
    return (segment, rows - first_rows, long_start)


class Swap:
    def __init__(self, part, *earlier):
        self.mine = after(low(part), *earlier)
        self.other = lax.ppermute(self.mine, "tensor", [(0, 1), (1, 0)])

    def total(self, *earlier):
        return wide(self.mine) + wide(after(self.other, *earlier))


class Halving:
    def __init__(self, grad, group_total, group_index, send_type=jnp.bfloat16):
        self.group_total = group_total
        self.group_index = group_index
        self.send_type = send_type
        self.bits = group_total.bit_length() - 1
        self.bit = 0
        rows = grad.shape[0] // group_total
        self.value = grad.reshape((2,) * self.bits + (rows,) + grad.shape[1:])
        self.prepare()

    def prepare(self):
        if self.bit < self.bits:
            axis = self.bits - 1 - self.bit
            mine = (self.group_index >> self.bit) & 1
            send = lax.dynamic_index_in_dim(self.value, 1 - mine, axis, keepdims=False)
            self.send = send.astype(self.send_type)
            self.keep = lax.dynamic_index_in_dim(self.value, mine, axis, keepdims=False)

    def stage(self, *earlier):
        if self.bit == self.bits:
            return self.value
        bit, self.bit = self.bit, self.bit + 1
        pairs = [(device, device ^ (1 << bit)) for device in range(self.group_total)]
        got = lax.ppermute(self.send, "dp", pairs)
        self.value = self.keep + wide(after(got, *earlier))
        self.prepare()
        return got

    def finish(self):
        while self.bit < self.bits:
            self.stage()
        return self.value


def after(value, *earlier):
    return lax.optimization_barrier((value,) + earlier)[0]


def scores_of(queries, keys, allowed):
    scores = (
        jnp.einsum("qhe,khe->hqk", queries, keys, preferred_element_type=jnp.float32) * SCORE_SCALE
    )
    if allowed is not None:
        scores = jnp.where(allowed, scores, MASK_FILL)
    return scores


def on_device(
    tokens,
    cotangent,
    attn_gain,
    mlp_gain,
    w_qkv,
    w_out,
    w_in,
    w_down,
    seq_lengths,
    set_owner,
    arrival,
):
    group_total = lax.axis_size("dp")
    group_index = lax.axis_index("dp")
    row_count = tokens.shape[0]
    model_width = tokens.shape[1]
    piece_count = arrival.shape[0] // group_total
    piece_rows = row_count // piece_count
    pair_cap = max(2, piece_count // group_total)
    slot_count = group_total * pair_cap
    target = arrival.reshape(group_total, piece_count)
    target_group = target // piece_count
    target_place = target % piece_count
    piece_ids = jnp.arange(piece_count, dtype=jnp.int32)
    earlier = piece_ids[None, :] < piece_ids[:, None]
    same_group = target_group[:, :, None] == target_group[:, None, :]
    slot_rank = jnp.sum((same_group & earlier[None]).astype(jnp.int32), axis=2)
    send_slot = target_group * pair_cap + slot_rank
    own_slots = lax.dynamic_index_in_dim(send_slot, group_index, 0, keepdims=False)
    slot_ids = jnp.arange(slot_count, dtype=jnp.int32)
    outgoing = own_slots[None, :] == slot_ids[:, None]
    out_piece = jnp.sum(jnp.where(outgoing, piece_ids[None, :], 0), axis=1)
    toward = target_group == group_index
    rank_ids = jnp.arange(pair_cap, dtype=jnp.int32)
    incoming = toward[:, None, :] & (slot_rank[:, None, :] == rank_ids[None, :, None])
    in_place = jnp.sum(jnp.where(incoming, target_place[:, None, :], 0), axis=2).reshape(slot_count)
    in_live = jnp.any(incoming, axis=2).reshape(slot_count)
    chosen = (in_place[None, :] == piece_ids[:, None]) & in_live[None, :]
    in_slot = jnp.sum(jnp.where(chosen, slot_ids[None, :], 0), axis=1)

    def take_pieces(values, ids, count):
        return (
            values.reshape(count, piece_rows, model_width)
            .at[ids]
            .get(mode="promise_in_bounds")
            .reshape(-1, model_width)
        )

    def deal(values):
        return lax.all_to_all(values, "dp", split_axis=0, concat_axis=0, tiled=True)

    held = set_owner == group_index
    lengths_mine = jnp.sum(jnp.where(held[:, None], seq_lengths, 0), axis=0)
    segment, position, long_start = segments(lengths_mine, row_count)
    half = row_count // 2
    low_first = jnp.arange(half, dtype=jnp.int32) < long_start

    def split(values):
        mask = low_first.reshape((half,) + (1,) * (values.ndim - 1))
        first, second = (values[:half], values[half:])
        return (jnp.where(mask, first, second), jnp.where(mask, second, first))

    def join(rest, long):
        mask = low_first.reshape((half,) + (1,) * (rest.ndim - 1))
        return jnp.concatenate([jnp.where(mask, rest, long), jnp.where(mask, long, rest)], axis=0)

    tokens_in = deal(take_pieces(tokens, out_piece, piece_count))
    inputs_pair = split(take_pieces(tokens_in, in_slot, slot_count))
    position_pair = split(position)
    seg_rest, _ = split(segment)
    allowed_rest = (seg_rest[:, None] == seg_rest[None, :])[None]
    features = w_qkv.shape[2]
    heads_local = features // HEAD

    saved = []
    for index in range(2):
        inputs = wide(inputs_pair[index])
        cosine, sine = rotary(position_pair[index])
        allowed = allowed_rest if index == 0 else None
        unit_one, scale_one = norm_parts(inputs)
        normed_one = low(unit_one * attn_gain)
        mixed = jnp.einsum("td,dcf->tcf", normed_one, w_qkv, preferred_element_type=jnp.float32)
        queries = low(spin(mixed[:, 0].reshape(half, heads_local, HEAD), cosine, sine))
        keys = low(spin(mixed[:, 1].reshape(half, heads_local, HEAD), cosine, sine))
        content = low(mixed[:, 2].reshape(half, heads_local, HEAD))
        scores = scores_of(queries, keys, allowed)
        highest = jnp.max(scores, axis=-1, keepdims=True)
        raised = jnp.exp(scores - highest)
        summed = jnp.sum(raised, axis=-1, keepdims=True)
        probs = low(raised / summed)
        attended = low(
            jnp.einsum("hqk,khe->qhe", probs, content, preferred_element_type=jnp.float32)
        ).reshape(half, features)
        branch = jnp.dot(attended, w_out, preferred_element_type=jnp.float32)
        saved.append(
            dict(
                inputs=inputs,
                cosine=cosine,
                sine=sine,
                allowed=allowed,
                normed_one=normed_one,
                queries=queries,
                keys=keys,
                content=content,
                log_total=highest + jnp.log(summed),
                attended=attended,
                branch=branch,
            )
        )
        saved[index]["swap"] = Swap(branch)
    rest, long = saved
    grads_in = deal(take_pieces(cotangent, out_piece, piece_count))
    grads_in = after(grads_in, long["swap"].mine)
    grads_pair = split(take_pieces(grads_in, in_slot, slot_count))
    for index in range(2):
        kept = saved[index]
        grad_y = grads_pair[index]
        if index == 0:
            total = rest["swap"].total(long["swap"].mine)
        else:
            total = long["swap"].total(rest["swap"].mine)
        kept["hidden"] = kept["inputs"] + total
        unit_two, scale_two = norm_parts(kept["hidden"])
        normed_two = low(unit_two * mlp_gain)
        gate_up = jnp.einsum("td,dcf->tcf", normed_two, w_in, preferred_element_type=jnp.float32)
        inner, gate = (gate_up[:, 0], gate_up[:, 1])
        below = 0.5 + 0.5 * lax.erf(inner * ROOT_HALF)
        active = inner * below
        slope = below + inner * (ROOT_TWO_PI_INV * jnp.exp(-0.5 * inner * inner))
        product = low(active * gate)
        grad_product = jnp.einsum("td,fd->tf", grad_y, w_down, preferred_element_type=jnp.float32)
        grad_inner = low(grad_product * gate * slope)
        grad_gate = low(grad_product * active)
        part = jnp.einsum(
            "tf,df->td", grad_inner, w_in[:, 0], preferred_element_type=jnp.float32
        ) + jnp.einsum("tf,df->td", grad_gate, w_in[:, 1], preferred_element_type=jnp.float32)
        kept["swap"] = Swap(part)
        kept.update(
            normed_two=normed_two, product=product, grad_inner=grad_inner, grad_gate=grad_gate
        )

    def both(name):
        return jnp.concatenate([rest[name], long[name]], axis=0)

    def weight_grad(left, right):
        grad = lax.dot_general(
            left, right, (((0,), (0,)), ((), ())), preferred_element_type=jnp.float32
        )
        return Halving(grad, group_total, group_index)

    grads_both = jnp.concatenate(grads_pair, axis=0)
    grads_both, normed_both = lax.optimization_barrier(
        (grads_both, both("normed_two"), long["swap"].mine)
    )[:2]
    sums_two = [
        weight_grad(grads_both, both("product")),
        weight_grad(normed_both, both("grad_inner")),
        weight_grad(normed_both, both("grad_gate")),
    ]
    for kept in saved:
        product = after(kept["product"], long["swap"].mine)
        mlp_part = jnp.dot(product, w_down, preferred_element_type=jnp.float32)
        kept["mlp_swap"] = Swap(mlp_part, rest["swap"].other)

    for index in range(2):
        kept = saved[index]
        if index == 0:
            back = kept["swap"].total(
                long["swap"].mine, *[part.send for part in sums_two]
            )
        else:
            back = kept["swap"].total(
                rest["last_swap"].mine, *[part.stage() for part in sums_two]
            )
        unit_two, scale_two = norm_parts(kept["hidden"])
        kept["mlp_gain_grad"] = jnp.sum(back * unit_two, axis=0)
        grad_hidden = wide(grads_pair[index]) + norm_back(unit_two, scale_two, back * mlp_gain)
        grad_branch = low(grad_hidden)
        upstream = low(
            jnp.einsum("td,fd->tf", grad_branch, w_out, preferred_element_type=jnp.float32)
        ).reshape(half, heads_local, HEAD)
        queries, keys, content = (kept["queries"], kept["keys"], kept["content"])
        if index == 1:
            results = [half_rows["hidden"] + half_rows["mlp_swap"].total() for half_rows in saved]
            packed_y = take_pieces(low(join(*results)), in_place, piece_count)
            content = after(content, packed_y)
            home_y = deal(packed_y)
        probs = jnp.exp(scores_of(queries, keys, kept["allowed"]) - kept["log_total"])
        grad_probs = jnp.einsum(
            "qhe,khe->hqk", upstream, content, preferred_element_type=jnp.float32
        )
        weighted = jnp.sum(probs * grad_probs, axis=-1, keepdims=True)
        grad_scores = low(probs * (grad_probs - weighted))
        query_grad = (
            jnp.einsum("hqk,khe->qhe", grad_scores, keys, preferred_element_type=jnp.float32)
            * SCORE_SCALE
        )
        key_grad = (
            jnp.einsum("hqk,qhe->khe", grad_scores, queries, preferred_element_type=jnp.float32)
            * SCORE_SCALE
        )
        value_grad = jnp.einsum(
            "hqk,qhe->khe", low(probs), upstream, preferred_element_type=jnp.float32
        )
        grad_mixed = jnp.concatenate(
            [
                low(spin_back(query_grad, kept["cosine"], kept["sine"])).reshape(half, features),
                low(spin_back(key_grad, kept["cosine"], kept["sine"])).reshape(half, features),
                low(value_grad).reshape(half, features),
            ],
            axis=1,
        )
        part = jnp.einsum(
            "tf,df->td",
            grad_mixed,
            w_qkv.reshape(model_width, 3 * features),
            preferred_element_type=jnp.float32,
        )
        kept.update(grad_hidden=grad_hidden, grad_branch=grad_branch, grad_mixed=grad_mixed)
        kept["last_swap"] = Swap(part)
    normed_both = both("normed_one")
    sum_out = weight_grad(both("grad_branch"), both("attended"))
    sum_qkv = weight_grad(normed_both, both("grad_mixed"))
    for index in range(2):
        kept = saved[index]
        if index == 0:
            back = kept["last_swap"].total(sum_out.send, sum_qkv.send)
        else:
            back = kept["last_swap"].total(
                home_y,
                *[part.stage(long["last_swap"].mine) for part in sums_two + [sum_out, sum_qkv]],
            )
        unit_one, scale_one = norm_parts(kept["inputs"])
        kept["attn_gain_grad"] = jnp.sum(back * unit_one, axis=0)
        kept["grad_inputs"] = kept["grad_hidden"] + norm_back(unit_one, scale_one, back * attn_gain)

    packed_dx = take_pieces(
        low(join(rest["grad_inputs"], long["grad_inputs"])), in_place, piece_count
    )
    home_dx = deal(packed_dx)
    gains = jnp.stack(
        [
            (rest[name] + long[name]).reshape(group_total, -1)
            for name in ("attn_gain_grad", "mlp_gain_grad")
        ],
        axis=1,
    )
    gains = Halving(after(gains, packed_dx), group_total, group_index, jnp.float32)
    gains = gains.finish().reshape(2, -1)
    for part in (sum_out, sum_qkv):
        part.finish()
    for part in sums_two:
        part.stage()
        part.finish()
    shard_down, shard_inner, shard_gate = [part.value for part in sums_two]
    back_y = wide(take_pieces(home_y, own_slots, slot_count))
    back_dx = wide(take_pieces(after(home_dx, back_y), own_slots, slot_count))
    return (
        back_y,
        back_dx,
        gains[0],
        gains[1],
        sum_qkv.finish().reshape(-1, 3, features),
        sum_out.finish().T,
        jnp.stack([shard_inner, shard_gate], axis=1),
        shard_down.T,
    )


def solution(mesh):
    placed = (
        P("dp", None),
        P("dp", None),
        P(),
        P(),
        P(None, None, "tensor"),
        P("tensor", None),
        P(None, None, "tensor"),
        P("tensor", None),
        P(),
        P(),
        P(),
    )

    return jax.shard_map(
        on_device,
        mesh=mesh,
        in_specs=placed,
        out_specs=(
            P("dp", None),
            P("dp", None),
            P("dp"),
            P("dp"),
            P("dp", None, "tensor"),
            P("tensor", "dp"),
            P("dp", None, "tensor"),
            P("tensor", "dp"),
        ),
        check_vma=False,
    )
```

profile of v0, /device:TPU:0, one launch (start us, length us, event | category | flops | bytes accessed | tf_op | source)
XLA Modules:
  0.0 464.4 jit_solution(7401075019939060769)
XLA Ops:
  2.6 3.6 gather_fusion
  6.2 7.6 %all-to-all-start = ((bf16[16,64,1024]{2,1,0:T(8,128)(2,1)}), bf16[16,64,1024]{2,1,0:T(8,128)(2,1)}, u32[]{:S(2)}, u32[]{:S(2)}) async-start(bf16[16,64,1024]{2,1,0:T(8,128)(2,1)} %bitcast.358), calls=%async_computation | async-start | bytes 4194304 | tf_op jit(solution)/shard_map/all_to_all | solution.py:176
  14.6 3.6 gather_fusion.2
  18.2 4.6 copy.112
  29.8 25.0 %all-to-all-done = bf16[16,64,1024]{2,1,0:T(8,128)(2,1)} async-done(((bf16[16,64,1024]{2,1,0:T(8,128)(2,1)}), bf16[16,64,1024]{2,1,0:T(8,128)(2,1)}, u32[]{:S(2)}, u32[]{:S(2)}) %all-to-all-start) | async-done | bytes 2097184 | tf_op jit(solution)/shard_map/all_to_all | solution.py:176
  54.9 11.3 %all-to-all-start.1 = ((bf16[16,64,1024]{2,1,0:T(8,128)(2,1)}), bf16[16,64,1024]{2,1,0:T(8,128)(2,1)}, u32[]{:S(2)}, u32[]{:S(2)}) async-start(bf16[16,64,1024]{2,1,0:T(8,128)(2,1)} %bitcast.357), calls=%async_computation.1 | async-start | bytes 4194304 | tf_op jit(solution)/shard_map/all_to_all | solution.py:176
  66.1 3.6 gather_fusion.1
  72.3 2.9 fusion.88
  77.0 4.0 fusion.81
  107.2 3.6 gather_fusion.3
  113.1 7.4 %collective-permute-done = bf16[512,1024]{1,0:T(8,128)(2,1)} collective-permute-done((bf16[512,1024]{1,0:T(8,128)(2,1)}, bf16[512,1024]{1,0:T(8,128)(2,1)}, u32[]{:S(2)}, u32[]{:S(2)}) %collective-permute-start) | collective-permute-done | bytes 1048608 | tf_op jit(solution)/shard_map/ppermute | solution.py:72
  123.8 3.0 fusion.155
  126.8 3.1 fusion.30
  135.1 7.9 %collective-permute-done.1 = bf16[512,1024]{1,0:T(8,128)(2,1)} collective-permute-done((bf16[512,1024]{1,0:T(8,128)(2,1)}, bf16[512,1024]{1,0:T(8,128)(2,1)}, u32[]{:S(2)}, u32[]{:S(2)}) %collective-permute-start.1) | collective-permute-done | bytes 1048608 | tf_op jit(solution)/shard_map/ppermute | solution.py:72
  146.0 3.0 fusion.153
  149.0 3.3 fusion.36
  157.6 3.5 fusion.45
  161.1 3.5 fusion.41
  168.4 3.9 fusion.37
  173.7 2.9 convolution_convert_fusion.1
  194.8 2.8 fusion.124
  216.5 16.4 %collective-permute-done.3 = bf16[512,1024]{1,0:T(8,128)(2,1)} collective-permute-done((bf16[512,1024]{1,0:T(8,128)(2,1)}, bf16[512,1024]{1,0:T(8,128)(2,1)}, u32[]{:S(2)}, u32[]{:S(2)}) %collective-permute-start.3) | collective-permute-done | bytes 1048608 | tf_op jit(solution)/shard_map/ppermute | solution.py:72
  232.9 4.5 fusion.213
  242.7 6.1 %all-to-all-start.2 = ((bf16[16,64,1024]{2,1,0:T(8,128)(2,1)}), bf16[16,64,1024]{2,1,0:T(8,128)(2,1)}, u32[]{:S(2)}, u32[]{:S(2)}) async-start(bf16[16,64,1024]{2,1,0:T(8,128)(2,1)} %bitcast.40), calls=%async_computation.2 | async-start | bytes 4194304 | tf_op jit(solution)/shard_map/all_to_all | solution.py:176
  248.9 5.1 %fusion.135 = bf16[8,64,512]{2,1,0:T(8,128)(2,1)S(1)} fusion(bf16[512,8,64]{0,2,1:T(8,128)(2,1)S(1)} %bitcast.379, f32[8,512,512]{1,2,0:T(8,128)} %copy-done.2, f32[8,512]{1,0:T(8,128)S(1)} %log_add_fusion), kind=kOutput, calls=%fused_computation.217 | convolution fusion | flops 274989056 | bytes 9453568 | tf_op jit(solution)/shard_map/hqk,qhe->khe/dot_general | solution.py:328
  254.0 4.7 %multiply_reduce_fusion = (f32[8,512]{1,0:T(8,128)S(1)}, f32[8,512,512]{1,2,0:T(8,128)S(1)}) fusion(f32[8,512,512]{1,2,0:T(8,128)} %copy-done.2, f32[8,512]{1,0:T(8,128)S(1)} %log_add_fusion, bf16[512,8,64]{0,2,1:T(8,128)(2,1)S(1)} %bitcast.380, bf16[512,8,64]{0,2,1:T(8,128)(2,1)S(1)} %bitcast.382), kind=kOutput, calls=%fused_computation.9 | convolution fusion | flops 276819968 | bytes 17858560 | tf_op jit(solution)/shard_map/qhe,khe->hqk/dot_general | solution.py:315
  273.0 3.5 fusion.13
  282.6 12.8 %collective-permute-done.30 = bf16[2,64,1312]{2,1,0:T(8,128)(2,1)S(1)} collective-permute-done((bf16[2,64,1312]{2,1,0:T(8,128)(2,1)S(1)}, bf16[2,64,1312]{2,1,0:T(8,128)(2,1)S(1)}, u32[]{:S(2)}, u32[]{:S(2)}) %collective-permute-start.30) | collective-permute-done | bytes 335904 | tf_op jit(solution)/shard_map/ppermute | solution.py:102
  295.5 4.6 collective-permute-start.31
  300.1 6.9 %collective-permute-done.28 = bf16[2,64,1312]{2,1,0:T(8,128)(2,1)S(1)} collective-permute-done((bf16[2,64,1312]{2,1,0:T(8,128)(2,1)S(1)}, bf16[2,64,1312]{2,1,0:T(8,128)(2,1)S(1)}, u32[]{:S(2)}, u32[]{:S(2)}) %collective-permute-start.28) | collective-permute-done | bytes 335904 | tf_op jit(solution)/shard_map/ppermute | solution.py:102
  307.1 4.6 collective-permute-start.29
  314.3 8.9 %collective-permute-start.27 = (bf16[64,1312]{1,0:T(8,128)(2,1)S(1)}, bf16[64,1312]{1,0:T(8,128)(2,1)S(1)}, u32[]{:S(2)}, u32[]{:S(2)}) collective-permute-start(bf16[64,1312]{1,0:T(8,128)(2,1)S(1)} %fusion.175), channel_id=1, source_target_pairs={{0,16},{2,18},{4,20},{6,22},{8,24},{10,26},{12,28},{14,30},{16,0},... | collective-permute-start | bytes 503816 | tf_op jit(solution)/shard_map/ppermute | solution.py:102
  325.0 6.8 %collective-permute-done.27 = bf16[64,1312]{1,0:T(8,128)(2,1)S(1)} collective-permute-done((bf16[64,1312]{1,0:T(8,128)(2,1)S(1)}, bf16[64,1312]{1,0:T(8,128)(2,1)S(1)}, u32[]{:S(2)}, u32[]{:S(2)}) %collective-permute-start.27) | collective-permute-done | bytes 167968 | tf_op jit(solution)/shard_map/ppermute | solution.py:102
  334.0 7.6 %collective-permute-done.23 = bf16[2,2,64,512]{3,2,0,1:T(8,128)(2,1)S(1)} collective-permute-done((bf16[2,2,64,512]{3,2,0,1:T(8,128)(2,1)S(1)}, bf16[2,2,64,512]{3,2,0,1:T(8,128)(2,1)S(1)}, u32[]{:S(2)}, u32[]{:S(2)}) %collective-permute-start.23) | collective-permute-done | bytes 262176 | tf_op jit(solution)/shard_map/ppermute | solution.py:102
  343.1 3.6 collective-permute-done.24
  350.8 3.8 fusion.86
  354.9 3.0 bitcast_add_fusion
  361.1 3.9 select_convert_fusion.1
  369.3 11.5 %collective-permute-done.17 = f32[2,2,1,2,64]{4,3,1,0,2:T(2,128)S(1)} collective-permute-done((f32[2,2,1,2,64]{4,3,1,0,2:T(2,128)S(1)}, f32[2,2,1,2,64]{4,3,1,0,2:T(2,128)S(1)}, u32[]{:S(2)}, u32[]{:S(2)}) %collective-permute-start.17) | collective-permute-done | bytes 2080 | tf_op jit(solution)/shard_map/ppermute | solution.py:102
  380.8 4.4 all-to-all-start.3
  388.8 31.3 %collective-permute-done.18 = f32[2,1,2,64]{3,2,1,0:T(2,128)S(1)} collective-permute-done((f32[2,1,2,64]{3,2,1,0:T(2,128)S(1)}, f32[2,1,2,64]{3,2,1,0:T(2,128)S(1)}, u32[]{:S(2)}, u32[]{:S(2)}) %collective-permute-start.18) | collective-permute-done | bytes 1056 | tf_op jit(solution)/shard_map/ppermute | solution.py:102
  420.1 4.5 collective-permute-start.19
  427.3 6.9 %collective-permute-done.19 = f32[1,2,64]{2,1,0:T(2,128)S(1)} collective-permute-done((f32[1,2,64]{2,1,0:T(2,128)S(1)}, f32[1,2,64]{2,1,0:T(2,128)S(1)}, u32[]{:S(2)}, u32[]{:S(2)}) %collective-permute-start.19) | collective-permute-done | bytes 544 | tf_op jit(solution)/shard_map/ppermute | solution.py:102
  434.2 3.1 collective-permute-done.21
  437.4 4.1 collective-permute-start.22
  442.0 8.1 %collective-permute-done.22 = bf16[64,1536]{1,0:T(8,128)(2,1)S(1)} collective-permute-done((bf16[64,1536]{1,0:T(8,128)(2,1)S(1)}, bf16[64,1536]{1,0:T(8,128)(2,1)S(1)}, u32[]{:S(2)}, u32[]{:S(2)}) %collective-permute-start.22) | collective-permute-done | bytes 196640 | tf_op jit(solution)/shard_map/ppermute | solution.py:102
  455.9 3.9 gather_fusion.7
  459.8 4.1 bitcast_convert_fusion
  (444 shorter events, 158.4 us)
Async XLA Ops:
  0.6 126.2 %copy-start = (bf16[1312,1024]{1,0:T(8,128)(2,1)S(1)}, bf16[1312,1024]{1,0:T(8,128)(2,1)}, u32[]{:S(2)}) copy-start(bf16[1312,1024]{1,0:T(8,128)(2,1)} %param.18) | copy-start | bytes 8060932
  6.2 48.6 %all-to-all-start = ((bf16[16,64,1024]{2,1,0:T(8,128)(2,1)}), bf16[16,64,1024]{2,1,0:T(8,128)(2,1)}, u32[]{:S(2)}, u32[]{:S(2)}) async-start(bf16[16,64,1024]{2,1,0:T(8,128)(2,1)} %bitcast.358), calls=%async_computation | async-start | bytes 4194304 | tf_op jit(solution)/shard_map/all_to_all | solution.py:176
  54.9 52.3 %all-to-all-start.1 = ((bf16[16,64,1024]{2,1,0:T(8,128)(2,1)}), bf16[16,64,1024]{2,1,0:T(8,128)(2,1)}, u32[]{:S(2)}, u32[]{:S(2)}) async-start(bf16[16,64,1024]{2,1,0:T(8,128)(2,1)} %bitcast.357), calls=%async_computation.1 | async-start | bytes 4194304 | tf_op jit(solution)/shard_map/all_to_all | solution.py:176
  94.2 26.3 %collective-permute-start = (bf16[512,1024]{1,0:T(8,128)(2,1)}, bf16[512,1024]{1,0:T(8,128)(2,1)}, u32[]{:S(2)}, u32[]{:S(2)}) collective-permute-start(bf16[512,1024]{1,0:T(8,128)(2,1)} %convolution_convert_fusion.3), channel_id=1, source_target_pairs={{0,1},{1,0},{2,3},{3,2},{4,5},{5,4},{6,7},{7,6},{8,9},{9,8},{10,11... | collective-permute-start | bytes 3145736 | tf_op jit(solution)/shard_map/ppermute | solution.py:72
  105.8 37.2 %collective-permute-start.1 = (bf16[512,1024]{1,0:T(8,128)(2,1)}, bf16[512,1024]{1,0:T(8,128)(2,1)}, u32[]{:S(2)}, u32[]{:S(2)}) collective-permute-start(bf16[512,1024]{1,0:T(8,128)(2,1)} %convolution_convert_fusion.2), channel_id=1, source_target_pairs={{0,1},{1,0},{2,3},{3,2},{4,5},{5,4},{6,7},{7,6},{8,9},{9,8},{10,11... | collective-permute-start | bytes 3145736 | tf_op jit(solution)/shard_map/ppermute | solution.py:72
  112.9 36.2 %copy-start.14 = (bf16[512,1024]{1,0:T(8,128)(2,1)}, bf16[512,1024]{1,0:T(8,128)(2,1)S(1)}, u32[]{:S(2)}) copy-start(bf16[512,1024]{1,0:T(8,128)(2,1)S(1)} %get-tuple-element.128) | copy-start | bytes 3145732
  122.7 58.2 %copy-start.4 = (f32[512,1024]{1,0:T(8,128)}, f32[512,1024]{1,0:T(8,128)S(1)}, u32[]{:S(2)}) copy-start(f32[512,1024]{1,0:T(8,128)S(1)} %get-tuple-element.106) | copy-start | bytes 6291460
  133.6 45.8 %collective-permute-start.2 = (bf16[512,1024]{1,0:T(8,128)(2,1)S(1)}, bf16[512,1024]{1,0:T(8,128)(2,1)S(1)}, u32[]{:S(2)}, u32[]{:S(2)}) collective-permute-start(bf16[512,1024]{1,0:T(8,128)(2,1)S(1)} %add_convert_fusion.1), channel_id=1, source_target_pairs={{0,1},{1,0},{2,3},{3,2},{4,5},{5,4},{6,7},{7,6},{8,9},{9,8},{10,11... | collective-permute-start | bytes 3145736 | tf_op jit(solution)/shard_map/ppermute | solution.py:72
  145.0 63.2 %copy-start.6 = (f32[512,1024]{1,0:T(8,128)}, f32[512,1024]{1,0:T(8,128)S(1)}, u32[]{:S(2)}) copy-start(f32[512,1024]{1,0:T(8,128)S(1)} %get-tuple-element.104) | copy-start | bytes 6291460
  156.0 52.2 %copy-start.32 = (bf16[512,1024]{1,0:T(8,128)(2,1)}, bf16[512,1024]{1,0:T(8,128)(2,1)S(1)}, u32[]{:S(2)}) copy-start(bf16[512,1024]{1,0:T(8,128)(2,1)S(1)} %add_convert_fusion) | copy-start | bytes 3145732
  156.0 50.2 %collective-permute-start.6 = (bf16[512,1024]{1,0:T(8,128)(2,1)S(1)}, bf16[512,1024]{1,0:T(8,128)(2,1)S(1)}, u32[]{:S(2)}, u32[]{:S(2)}) collective-permute-start(bf16[512,1024]{1,0:T(8,128)(2,1)S(1)} %add_convert_fusion), channel_id=1, source_target_pairs={{0,1},{1,0},{2,3},{3,2},{4,5},{5,4},{6,7},{7,6},{8,9},{9,8},{10,11... | collective-permute-start | bytes 3145736 | tf_op jit(solution)/shard_map/ppermute | solution.py:72
  167.8 29.8 %collective-permute-start.9 = (bf16[2,2,2,64,1312]{4,3,2,1,0:T(8,128)(2,1)}, bf16[2,2,2,64,1312]{4,3,2,1,0:T(8,128)(2,1)}, u32[]{:S(2)}, u32[]{:S(2)}) collective-permute-start(bf16[2,2,2,64,1312]{4,3,2,1,0:T(8,128)(2,1)} %fusion.129), channel_id=1, source_target_pairs={{0,2},{2,0},{4,6},{6,4},{8,10},{10,8},{12,14},{14,12},{16,18},{18,... | collective-permute-start | bytes 4030472 | tf_op jit(solution)/shard_map/ppermute | solution.py:102
  167.8 33.1 %collective-permute-start.8 = (bf16[2,2,2,64,1312]{4,3,2,1,0:T(8,128)(2,1)}, bf16[2,2,2,64,1312]{4,3,2,1,0:T(8,128)(2,1)}, u32[]{:S(2)}, u32[]{:S(2)}) collective-permute-start(bf16[2,2,2,64,1312]{4,3,2,1,0:T(8,128)(2,1)} %fusion.128), channel_id=1, source_target_pairs={{0,2},{2,0},{4,6},{6,4},{8,10},{10,8},{12,14},{14,12},{16,18},{18,... | collective-permute-start | bytes 4030472 | tf_op jit(solution)/shard_map/ppermute | solution.py:102
  173.7 34.3 %collective-permute-start.7 = (bf16[2,2,2,64,1312]{4,3,2,1,0:T(8,128)(2,1)}, bf16[2,2,2,64,1312]{4,3,2,1,0:T(8,128)(2,1)}, u32[]{:S(2)}, u32[]{:S(2)}) collective-permute-start(bf16[2,2,2,64,1312]{4,3,2,1,0:T(8,128)(2,1)} %fusion.127), channel_id=1, source_target_pairs={{0,2},{2,0},{4,6},{6,4},{8,10},{10,8},{12,14},{14,12},{16,18},{18,... | collective-permute-start | bytes 4030472 | tf_op jit(solution)/shard_map/ppermute | solution.py:102
  179.4 35.2 %collective-permute-start.4 = (bf16[512,1024]{1,0:T(8,128)(2,1)}, bf16[512,1024]{1,0:T(8,128)(2,1)}, u32[]{:S(2)}, u32[]{:S(2)}) collective-permute-start(bf16[512,1024]{1,0:T(8,128)(2,1)} %convolution_convert_fusion), channel_id=1, source_target_pairs={{0,1},{1,0},{2,3},{3,2},{4,5},{5,4},{6,7},{7,6},{8,9},{9,8},{10,11... | collective-permute-start | bytes 3145736 | tf_op jit(solution)/shard_map/ppermute | solution.py:72
  197.6 35.3 %collective-permute-start.3 = (bf16[512,1024]{1,0:T(8,128)(2,1)}, bf16[512,1024]{1,0:T(8,128)(2,1)}, u32[]{:S(2)}, u32[]{:S(2)}) collective-permute-start(bf16[512,1024]{1,0:T(8,128)(2,1)} %convolution_convert_fusion.1), channel_id=1, source_target_pairs={{0,1},{1,0},{2,3},{3,2},{4,5},{5,4},{6,7},{7,6},{8,9},{9,8},{10,11... | collective-permute-start | bytes 3145736 | tf_op jit(solution)/shard_map/ppermute | solution.py:72
  200.9 122.5 %collective-permute-start.5 = (bf16[512,1024]{1,0:T(8,128)(2,1)}, bf16[512,1024]{1,0:T(8,128)(2,1)}, u32[]{:S(2)}, u32[]{:S(2)}) collective-permute-start(bf16[512,1024]{1,0:T(8,128)(2,1)} %fusion.124), channel_id=1, source_target_pairs={{0,1},{1,0},{2,3},{3,2},{4,5},{5,4},{6,7},{7,6},{8,9},{9,8},{10,11... | collective-permute-start | bytes 3145736 | tf_op jit(solution)/shard_map/ppermute | solution.py:72
  206.2 62.4 %collective-permute-start.13 = (bf16[2,2,64,1312]{3,2,1,0:T(8,128)(2,1)}, bf16[2,2,64,1312]{3,2,1,0:T(8,128)(2,1)}, u32[]{:S(2)}, u32[]{:S(2)}) collective-permute-start(bf16[2,2,64,1312]{3,2,1,0:T(8,128)(2,1)} %fusion.164), channel_id=1, source_target_pairs={{0,4},{2,6},{4,0},{6,2},{8,12},{10,14},{12,8},{14,10},{16,20},{18,... | collective-permute-start | bytes 2015240 | tf_op jit(solution)/shard_map/ppermute | solution.py:102
  208.0 68.5 %collective-permute-start.12 = (bf16[2,2,64,1312]{3,2,1,0:T(8,128)(2,1)}, bf16[2,2,64,1312]{3,2,1,0:T(8,128)(2,1)}, u32[]{:S(2)}, u32[]{:S(2)}) collective-permute-start(bf16[2,2,64,1312]{3,2,1,0:T(8,128)(2,1)} %fusion.163), channel_id=1, source_target_pairs={{0,4},{2,6},{4,0},{6,2},{8,12},{10,14},{12,8},{14,10},{16,20},{18,... | collective-permute-start | bytes 2015240 | tf_op jit(solution)/shard_map/ppermute | solution.py:102
  209.3 23.6 %copy-start.5 = (f32[512,1024]{1,0:T(8,128)S(1)}, f32[512,1024]{1,0:T(8,128)}, u32[]{:S(2)}) copy-start(f32[512,1024]{1,0:T(8,128)} %copy-done.4) | copy-start | bytes 6291460
  209.3 23.6 %copy-start.7 = (f32[512,1024]{1,0:T(8,128)S(1)}, f32[512,1024]{1,0:T(8,128)}, u32[]{:S(2)}) copy-start(f32[512,1024]{1,0:T(8,128)} %copy-done.6) | copy-start | bytes 6291460
  209.3 23.6 %copy-start.33 = (bf16[512,1024]{1,0:T(8,128)(2,1)S(1)}, bf16[512,1024]{1,0:T(8,128)(2,1)}, u32[]{:S(2)}) copy-start(bf16[512,1024]{1,0:T(8,128)(2,1)} %copy-done.32) | copy-start | bytes 3145732
  209.3 23.6 %copy-start.35 = (bf16[512,1024]{1,0:T(8,128)(2,1)S(1)}, bf16[512,1024]{1,0:T(8,128)(2,1)}, u32[]{:S(2)}) copy-start(bf16[512,1024]{1,0:T(8,128)(2,1)} %copy-done.34) | copy-start | bytes 3145732
  214.5 22.9 %copy-start.89 = (bf16[8,64,512]{2,1,0:T(8,128)(2,1)S(1)}, bf16[8,64,512]{2,1,0:T(8,128)(2,1)}, u32[]{:S(2)}) copy-start(bf16[8,64,512]{2,1,0:T(8,128)(2,1)} %copy-done.88) | copy-start | bytes 1572868
  214.6 54.0 %collective-permute-start.11 = (bf16[2,2,64,1312]{3,2,1,0:T(8,128)(2,1)}, bf16[2,2,64,1312]{3,2,1,0:T(8,128)(2,1)}, u32[]{:S(2)}, u32[]{:S(2)}) collective-permute-start(bf16[2,2,64,1312]{3,2,1,0:T(8,128)(2,1)} %fusion.162), channel_id=1, source_target_pairs={{0,4},{2,6},{4,0},{6,2},{8,12},{10,14},{12,8},{14,10},{16,20},{18,... | collective-permute-start | bytes 2015240 | tf_op jit(solution)/shard_map/ppermute | solution.py:102
  240.4 92.2 %collective-permute-start.14 = (bf16[2,2,2,64,512]{4,3,0,1,2:T(8,128)(2,1)}, bf16[2,2,2,64,512]{4,3,0,1,2:T(8,128)(2,1)}, u32[]{:S(2)}, u32[]{:S(2)}) collective-permute-start(bf16[2,2,2,64,512]{4,3,0,1,2:T(8,128)(2,1)} %fusion.165), channel_id=1, source_target_pairs={{0,2},{2,0},{4,6},{6,4},{8,10},{10,8},{12,14},{14,12},{16,18},{18,... | collective-permute-start | bytes 1572872 | tf_op jit(solution)/shard_map/ppermute | solution.py:102
  242.7 138.1 %all-to-all-start.2 = ((bf16[16,64,1024]{2,1,0:T(8,128)(2,1)}), bf16[16,64,1024]{2,1,0:T(8,128)(2,1)}, u32[]{:S(2)}, u32[]{:S(2)}) async-start(bf16[16,64,1024]{2,1,0:T(8,128)(2,1)} %bitcast.40), calls=%async_computation.2 | async-start | bytes 4194304 | tf_op jit(solution)/shard_map/all_to_all | solution.py:176
  268.5 82.2 %copy-start.30 = (bf16[512,1024]{1,0:T(8,128)(2,1)}, bf16[512,1024]{1,0:T(8,128)(2,1)S(1)}, u32[]{:S(2)}) copy-start(bf16[512,1024]{1,0:T(8,128)(2,1)S(1)} %fusion.121) | copy-start | bytes 3145732
  276.5 46.7 %copy-start.38 = (f32[1024,1536]{1,0:T(8,128)}, f32[1024,1536]{1,0:T(8,128)S(1)}, u32[]{:S(2)}) copy-start(f32[1024,1536]{1,0:T(8,128)S(1)} %fusion.13) | copy-start | bytes 18874372
  278.4 17.0 %collective-permute-start.30 = (bf16[2,64,1312]{2,1,0:T(8,128)(2,1)S(1)}, bf16[2,64,1312]{2,1,0:T(8,128)(2,1)S(1)}, u32[]{:S(2)}, u32[]{:S(2)}) collective-permute-start(bf16[2,64,1312]{2,1,0:T(8,128)(2,1)S(1)} %fusion.169), channel_id=1, source_target_pairs={{0,8},{2,10},{4,12},{6,14},{8,0},{10,2},{12,4},{14,6},{16,24},{18,... | collective-permute-start | bytes 1007624 | tf_op jit(solution)/shard_map/ppermute | solution.py:102
  280.4 26.6 %collective-permute-start.28 = (bf16[2,64,1312]{2,1,0:T(8,128)(2,1)S(1)}, bf16[2,64,1312]{2,1,0:T(8,128)(2,1)S(1)}, u32[]{:S(2)}, u32[]{:S(2)}) collective-permute-start(bf16[2,64,1312]{2,1,0:T(8,128)(2,1)S(1)} %fusion.168), channel_id=1, source_target_pairs={{0,8},{2,10},{4,12},{6,14},{8,0},{10,2},{12,4},{14,6},{16,24},{18,... | collective-permute-start | bytes 1007624 | tf_op jit(solution)/shard_map/ppermute | solution.py:102
  280.6 33.5 %collective-permute-start.26 = (bf16[2,64,1312]{2,1,0:T(8,128)(2,1)S(1)}, bf16[2,64,1312]{2,1,0:T(8,128)(2,1)S(1)}, u32[]{:S(2)}, u32[]{:S(2)}) collective-permute-start(bf16[2,64,1312]{2,1,0:T(8,128)(2,1)S(1)} %fusion.167), channel_id=1, source_target_pairs={{0,8},{2,10},{4,12},{6,14},{8,0},{10,2},{12,4},{14,6},{16,24},{18,... | collective-permute-start | bytes 1007624 | tf_op jit(solution)/shard_map/ppermute | solution.py:102
  295.5 29.5 %collective-permute-start.31 = (bf16[64,1312]{1,0:T(8,128)(2,1)S(1)}, bf16[64,1312]{1,0:T(8,128)(2,1)S(1)}, u32[]{:S(2)}, u32[]{:S(2)}) collective-permute-start(bf16[64,1312]{1,0:T(8,128)(2,1)S(1)} %fusion.177), channel_id=1, source_target_pairs={{0,16},{2,18},{4,20},{6,22},{8,24},{10,26},{12,28},{14,30},{16,0},... | collective-permute-start | bytes 503816 | tf_op jit(solution)/shard_map/ppermute | solution.py:102
  307.1 17.9 %collective-permute-start.29 = (bf16[64,1312]{1,0:T(8,128)(2,1)S(1)}, bf16[64,1312]{1,0:T(8,128)(2,1)S(1)}, u32[]{:S(2)}, u32[]{:S(2)}) collective-permute-start(bf16[64,1312]{1,0:T(8,128)(2,1)S(1)} %fusion.176), channel_id=1, source_target_pairs={{0,16},{2,18},{4,20},{6,22},{8,24},{10,26},{12,28},{14,30},{16,0},... | collective-permute-start | bytes 503816 | tf_op jit(solution)/shard_map/ppermute | solution.py:102
  314.3 17.5 %collective-permute-start.27 = (bf16[64,1312]{1,0:T(8,128)(2,1)S(1)}, bf16[64,1312]{1,0:T(8,128)(2,1)S(1)}, u32[]{:S(2)}, u32[]{:S(2)}) collective-permute-start(bf16[64,1312]{1,0:T(8,128)(2,1)S(1)} %fusion.175), channel_id=1, source_target_pairs={{0,16},{2,18},{4,20},{6,22},{8,24},{10,26},{12,28},{14,30},{16,0},... | collective-permute-start | bytes 503816 | tf_op jit(solution)/shard_map/ppermute | solution.py:102
  323.4 27.3 %collective-permute-start.10 = (bf16[512,1024]{1,0:T(8,128)(2,1)S(1)}, bf16[512,1024]{1,0:T(8,128)(2,1)S(1)}, u32[]{:S(2)}, u32[]{:S(2)}) collective-permute-start(bf16[512,1024]{1,0:T(8,128)(2,1)S(1)} %fusion.121), channel_id=1, source_target_pairs={{0,1},{1,0},{2,3},{3,2},{4,5},{5,4},{6,7},{7,6},{8,9},{9,8},{10,11... | collective-permute-start | bytes 3145736 | tf_op jit(solution)/shard_map/ppermute | solution.py:72
  325.0 24.6 %collective-permute-start.15 = (bf16[2,2,2,64,1536]{4,3,0,1,2:T(8,128)(2,1)S(1)}, bf16[2,2,2,64,1536]{4,3,0,1,2:T(8,128)(2,1)S(1)}, u32[]{:S(2)}, u32[]{:S(2)}) collective-permute-start(bf16[2,2,2,64,1536]{4,3,0,1,2:T(8,128)(2,1)S(1)} %fusion.104), channel_id=1, source_target_pairs={{0,2},{2,0},{4,6},{6,4},{8,10},{10,8},{12,14},{14,12},{16,18},{18,... | collective-permute-start | bytes 4718600 | tf_op jit(solution)/shard_map/ppermute | solution.py:102
  333.9 7.7 %collective-permute-start.23 = (bf16[2,2,64,512]{3,2,0,1:T(8,128)(2,1)S(1)}, bf16[2,2,64,512]{3,2,0,1:T(8,128)(2,1)S(1)}, u32[]{:S(2)}, u32[]{:S(2)}) collective-permute-start(bf16[2,2,64,512]{3,2,0,1:T(8,128)(2,1)S(1)} %fusion.173), channel_id=1, source_target_pairs={{0,4},{2,6},{4,0},{6,2},{8,12},{10,14},{12,8},{14,10},{16,20},{18,... | collective-permute-start | bytes 786440 | tf_op jit(solution)/shard_map/ppermute | solution.py:102
  341.8 5.0 %collective-permute-start.24 = (bf16[2,64,512]{2,1,0:T(8,128)(2,1)S(1)}, bf16[2,64,512]{2,1,0:T(8,128)(2,1)S(1)}, u32[]{:S(2)}, u32[]{:S(2)}) collective-permute-start(bf16[2,64,512]{2,1,0:T(8,128)(2,1)S(1)} %fusion.178), channel_id=1, source_target_pairs={{0,8},{2,10},{4,12},{6,14},{8,0},{10,2},{12,4},{14,6},{16,24},{18,... | collective-permute-start | bytes 393224 | tf_op jit(solution)/shard_map/ppermute | solution.py:102
  346.9 41.9 %collective-permute-start.25 = (bf16[64,512]{1,0:T(8,128)(2,1)S(1)}, bf16[64,512]{1,0:T(8,128)(2,1)S(1)}, u32[]{:S(2)}, u32[]{:S(2)}) collective-permute-start(bf16[64,512]{1,0:T(8,128)(2,1)S(1)} %fusion.180), channel_id=1, source_target_pairs={{0,16},{2,18},{4,20},{6,22},{8,24},{10,26},{12,28},{14,30},{16,0},... | collective-permute-start | bytes 196616 | tf_op jit(solution)/shard_map/ppermute | solution.py:102
  354.8 10.4 %collective-permute-start.16 = (f32[2,2,2,1,2,64]{5,4,2,1,0,3:T(2,128)S(1)}, f32[2,2,2,1,2,64]{5,4,2,1,0,3:T(2,128)S(1)}, u32[]{:S(2)}, u32[]{:S(2)}) collective-permute-start(f32[2,2,2,1,2,64]{5,4,2,1,0,3:T(2,128)S(1)} %bitcast.404), channel_id=1, source_target_pairs={{0,2},{2,0},{4,6},{6,4},{8,10},{10,8},{12,14},{14,12},{16,18},{18,... | collective-permute-start | bytes 12296 | tf_op jit(solution)/shard_map/ppermute | solution.py:102
  360.6 64.0 %collective-permute-start.20 = (bf16[2,2,64,1536]{3,2,0,1:T(8,128)(2,1)}, bf16[2,2,64,1536]{3,2,0,1:T(8,128)(2,1)}, u32[]{:S(2)}, u32[]{:S(2)}) collective-permute-start(bf16[2,2,64,1536]{3,2,0,1:T(8,128)(2,1)} %fusion.161), channel_id=1, source_target_pairs={{0,4},{2,6},{4,0},{6,2},{8,12},{10,14},{12,8},{14,10},{16,20},{18,... | collective-permute-start | bytes 2359304 | tf_op jit(solution)/shard_map/ppermute | solution.py:102
  365.3 15.6 %collective-permute-start.17 = (f32[2,2,1,2,64]{4,3,1,0,2:T(2,128)S(1)}, f32[2,2,1,2,64]{4,3,1,0,2:T(2,128)S(1)}, u32[]{:S(2)}, u32[]{:S(2)}) collective-permute-start(f32[2,2,1,2,64]{4,3,1,0,2:T(2,128)S(1)} %fusion.188), channel_id=1, source_target_pairs={{0,4},{2,6},{4,0},{6,2},{8,12},{10,14},{12,8},{14,10},{16,20},{18,... | collective-permute-start | bytes 6152 | tf_op jit(solution)/shard_map/ppermute | solution.py:102
  380.8 75.1 %all-to-all-start.3 = ((bf16[16,64,1024]{2,1,0:T(8,128)(2,1)}), bf16[16,64,1024]{2,1,0:T(8,128)(2,1)}, u32[]{:S(2)}, u32[]{:S(2)}) async-start(bf16[16,64,1024]{2,1,0:T(8,128)(2,1)} %bitcast.79), calls=%async_computation.3 | async-start | bytes 4194304 | tf_op jit(solution)/shard_map/all_to_all | solution.py:176
  385.3 34.8 %collective-permute-start.18 = (f32[2,1,2,64]{3,2,1,0:T(2,128)S(1)}, f32[2,1,2,64]{3,2,1,0:T(2,128)S(1)}, u32[]{:S(2)}, u32[]{:S(2)}) collective-permute-start(f32[2,1,2,64]{3,2,1,0:T(2,128)S(1)} %fusion.191), channel_id=1, source_target_pairs={{0,8},{2,10},{4,12},{6,14},{8,0},{10,2},{12,4},{14,6},{16,24},{18,... | collective-permute-start | bytes 3080 | tf_op jit(solution)/shard_map/ppermute | solution.py:102
  420.1 14.1 %collective-permute-start.19 = (f32[1,2,64]{2,1,0:T(2,128)S(1)}, f32[1,2,64]{2,1,0:T(2,128)S(1)}, u32[]{:S(2)}, u32[]{:S(2)}) collective-permute-start(f32[1,2,64]{2,1,0:T(2,128)S(1)} %fusion.194), channel_id=1, source_target_pairs={{0,16},{2,18},{4,20},{6,22},{8,24},{10,26},{12,28},{14,30},{16,0},... | collective-permute-start | bytes 1544 | tf_op jit(solution)/shard_map/ppermute | solution.py:102
  426.5 10.8 %collective-permute-start.21 = (bf16[2,64,1536]{2,1,0:T(8,128)(2,1)S(1)}, bf16[2,64,1536]{2,1,0:T(8,128)(2,1)S(1)}, u32[]{:S(2)}, u32[]{:S(2)}) collective-permute-start(bf16[2,64,1536]{2,1,0:T(8,128)(2,1)S(1)} %fusion.166), channel_id=1, source_target_pairs={{0,8},{2,10},{4,12},{6,14},{8,0},{10,2},{12,4},{14,6},{16,24},{18,... | collective-permute-start | bytes 1179656 | tf_op jit(solution)/shard_map/ppermute | solution.py:102
  437.4 12.7 %collective-permute-start.22 = (bf16[64,1536]{1,0:T(8,128)(2,1)S(1)}, bf16[64,1536]{1,0:T(8,128)(2,1)S(1)}, u32[]{:S(2)}, u32[]{:S(2)}) collective-permute-start(bf16[64,1536]{1,0:T(8,128)(2,1)S(1)} %fusion.174), channel_id=1, source_target_pairs={{0,16},{2,18},{4,20},{6,22},{8,24},{10,26},{12,28},{14,30},{16,0},... | collective-permute-start | bytes 589832 | tf_op jit(solution)/shard_map/ppermute | solution.py:102
  (92 other events, 508.6 us)
where the time goes:
time: 470 us; the launch traced here: 464 us
  waiting for transfers between devices  159 us (34%)
  starting transfers between devices  82.4 us (18%)
  other arithmetic  78.5 us (17%)
  matrix products  78.4 us (17%)
  local copies, waits for them, and re-layouts  63.2 us (13%)
    ppermute x24, waiting for transfers between devices, stage(): got = lax.ppermute(self.send, 'dp', pairs)  101 us
    ppermute x24, starting transfers between devices, stage(): got = lax.ppermute(self.send, 'dp', pairs)  43.6 us
    ppermute x8, waiting for transfers between devices, __init__(): self.other = lax.ppermute(self.mine, 'tensor', [(0, 1), (1, 0)])  31.7 us
    all_to_all x4, starting transfers between devices, deal(): return lax.all_to_all(values, 'dp', split_axis=0, concat_axis=0, tiled=True)  29.4 us
    all_to_all x4, waiting for transfers between devices, deal(): return lax.all_to_all(values, 'dp', split_axis=0, concat_axis=0, tiled=True)  25.9 us
    gather x8, local copies, waits for them, and re-layouts, take_pieces(): return values.reshape(count, piece_rows, model_width).at[ids].get(mode='p...  25 us
    unnamed x210, local copies, waits for them, and re-layouts  21.3 us
    convert_element_type x11, other arithmetic, low(): return values.astype(jnp.bfloat16)  19.4 us
  transfers between devices with their start and end apart: 36, of which 16 were waited for; matrix products, arithmetic and copies ran while one was open for 41% of the time, Pallas kernels for 0%

commit v1 on v0

--- a/solution.py
+++ b/solution.py
@@ -373,14 +373,15 @@
     )
     gains = Halving(after(gains, packed_dx), group_total, group_index, jnp.float32)
     gains = gains.finish().reshape(2, -1)
-    for part in (sum_out, sum_qkv):
-        part.finish()
+    back_y = wide(take_pieces(home_y, own_slots, slot_count))
+    back_dx = wide(take_pieces(after(home_dx, back_y), own_slots, slot_count))
+    while sum_qkv.bit < sum_qkv.bits:
+        sum_out.stage()
+        sum_qkv.stage(*([back_dx] if sum_qkv.bit == sum_qkv.bits - 2 else []))
     for part in sums_two:
         part.stage()
         part.finish()
     shard_down, shard_inner, shard_gate = [part.value for part in sums_two]
-    back_y = wide(take_pieces(home_y, own_slots, slot_count))
-    back_dx = wide(take_pieces(after(home_dx, back_y), own_slots, slot_count))
     return (
         back_y,
         back_dx,

time: 470 us -> 442 us (0.940)
  starting transfers between devices: 82.4 us -> 67.6 us
  waiting for transfers between devices: 159 us -> 151 us
    ppermute x24, starting transfers between devices: 43.6 us -> 28 us  [stage(): got = lax.ppermute(self.send, 'dp', pairs)]
    ppermute x24, waiting for transfers between devices: 101 us -> 93.1 us  [stage(): got = lax.ppermute(self.send, 'dp', pairs)]
    unnamed x210 -> x202, local copies, waits for them, and re-layouts: 21.3 us -> 18.1 us
  transfers between devices with their start and end apart: 36 -> 36, of which waited for: 16 -> 15; matrix products, arithmetic and copies ran while one was open for 41% -> 45% of each run, Pallas kernels for 0% -> 0%
where the time goes in v1:
time: 442 us; the launch traced here: 436 us
  waiting for transfers between devices  151 us (34%)
  matrix products  78.5 us (18%)
  other arithmetic  76.6 us (17%)
  starting transfers between devices  67.6 us (15%)
  local copies, waits for them, and re-layouts  59 us (13%)
    ppermute x24, waiting for transfers between devices, stage(): got = lax.ppermute(self.send, 'dp', pairs)  93.1 us
    ppermute x8, waiting for transfers between devices, __init__(): self.other = lax.ppermute(self.mine, 'tensor', [(0, 1), (1, 0)])  32.1 us
    all_to_all x4, starting transfers between devices, deal(): return lax.all_to_all(values, 'dp', split_axis=0, concat_axis=0, tiled=True)  29.7 us
    ppermute x24, starting transfers between devices, stage(): got = lax.ppermute(self.send, 'dp', pairs)  28 us
    all_to_all x4, waiting for transfers between devices, deal(): return lax.all_to_all(values, 'dp', split_axis=0, concat_axis=0, tiled=True)  25.8 us
    gather x8, local copies, waits for them, and re-layouts, take_pieces(): return values.reshape(count, piece_rows, model_width).at[ids].get(mode='p...  24.7 us
    convert_element_type x11, other arithmetic, low(): return values.astype(jnp.bfloat16)  19.4 us
    unnamed x202, local copies, waits for them, and re-layouts  18.1 us
  transfers between devices with their start and end apart: 36, of which 15 were waited for; matrix products, arithmetic and copies ran while one was open for 45% of the time, Pallas kernels for 0%

profile of v1, /device:TPU:0, one launch (start us, length us, event | category | flops | bytes accessed | tf_op | source)
XLA Modules:
  0.0 435.8 jit_solution(12571708943058679388)
XLA Ops:
  2.6 3.6 gather_fusion
  6.2 7.6 %all-to-all-start = ((bf16[16,64,1024]{2,1,0:T(8,128)(2,1)}), bf16[16,64,1024]{2,1,0:T(8,128)(2,1)}, u32[]{:S(2)}, u32[]{:S(2)}) async-start(bf16[16,64,1024]{2,1,0:T(8,128)(2,1)} %bitcast.358), calls=%async_computation | async-start | bytes 4194304 | tf_op jit(solution)/shard_map/all_to_all | solution.py:176
  14.6 3.6 gather_fusion.2
  18.2 4.6 %copy.112 = bf16[1024,3,512]{0,2,1:T(8,128)(2,1)} copy(bf16[1024,3,512]{2,0,1:T(8,128)(2,1)} %param.15) | data formatting | bytes 6291456 | tf_op args[4]
  29.8 25.0 %all-to-all-done = bf16[16,64,1024]{2,1,0:T(8,128)(2,1)} async-done(((bf16[16,64,1024]{2,1,0:T(8,128)(2,1)}), bf16[16,64,1024]{2,1,0:T(8,128)(2,1)}, u32[]{:S(2)}, u32[]{:S(2)}) %all-to-all-start) | async-done | bytes 2097184 | tf_op jit(solution)/shard_map/all_to_all | solution.py:176
  54.9 11.3 %all-to-all-start.1 = ((bf16[16,64,1024]{2,1,0:T(8,128)(2,1)}), bf16[16,64,1024]{2,1,0:T(8,128)(2,1)}, u32[]{:S(2)}, u32[]{:S(2)}) async-start(bf16[16,64,1024]{2,1,0:T(8,128)(2,1)} %bitcast.357), calls=%async_computation.1 | async-start | bytes 4194304 | tf_op jit(solution)/shard_map/all_to_all | solution.py:176
  66.1 3.6 gather_fusion.1
  72.3 2.9 fusion.88
  77.0 4.0 fusion.81
  107.2 3.6 gather_fusion.3
  113.1 7.5 %collective-permute-done = bf16[512,1024]{1,0:T(8,128)(2,1)} collective-permute-done((bf16[512,1024]{1,0:T(8,128)(2,1)}, bf16[512,1024]{1,0:T(8,128)(2,1)}, u32[]{:S(2)}, u32[]{:S(2)}) %collective-permute-start) | collective-permute-done | bytes 1048608 | tf_op jit(solution)/shard_map/ppermute | solution.py:72
  123.9 3.0 fusion.155
  126.9 3.1 fusion.30
  135.2 7.9 %collective-permute-done.1 = bf16[512,1024]{1,0:T(8,128)(2,1)} collective-permute-done((bf16[512,1024]{1,0:T(8,128)(2,1)}, bf16[512,1024]{1,0:T(8,128)(2,1)}, u32[]{:S(2)}, u32[]{:S(2)}) %collective-permute-start.1) | collective-permute-done | bytes 1048608 | tf_op jit(solution)/shard_map/ppermute | solution.py:72
  146.1 3.0 fusion.153
  149.1 3.3 fusion.36
  157.6 3.5 fusion.45
  161.1 3.5 fusion.41
  168.4 3.9 fusion.37
  173.8 2.9 convolution_convert_fusion.1
  176.7 2.8 convolution_convert_fusion
  194.9 2.8 fusion.124
  216.2 16.8 %collective-permute-done.3 = bf16[512,1024]{1,0:T(8,128)(2,1)} collective-permute-done((bf16[512,1024]{1,0:T(8,128)(2,1)}, bf16[512,1024]{1,0:T(8,128)(2,1)}, u32[]{:S(2)}, u32[]{:S(2)}) %collective-permute-start.3) | collective-permute-done | bytes 1048608 | tf_op jit(solution)/shard_map/ppermute | solution.py:72
  233.0 4.5 %fusion.213 = (bf16[512,1024]{1,0:T(8,128)(2,1)S(1)}, f32[512,1024]{1,0:T(8,128)}, bf16[512,1024]{1,0:T(8,128)(2,1)S(1)}, bf16[512,1024]{1,0:T(8,128)(2,1)S(1)}) fusion(f32[512]{0:T(512)S(1)} %broadcast_multiply_fusion.14, f32[512,1024]{1,0:T(8,128)S(1)} %copy-done.7, f32[512]{0:T(512)S(1)} %broadcast_multiply_fusion.18, ...), kind=kLoop, calls=%fused_computation.435 | loop fusion | flops 13107200 | bytes 16790016 | tf_op jit(solution)/shard_map/convert_element_type | solution.py:17
  242.8 6.1 %all-to-all-start.2 = ((bf16[16,64,1024]{2,1,0:T(8,128)(2,1)}), bf16[16,64,1024]{2,1,0:T(8,128)(2,1)}, u32[]{:S(2)}, u32[]{:S(2)}) async-start(bf16[16,64,1024]{2,1,0:T(8,128)(2,1)} %bitcast.40), calls=%async_computation.2 | async-start | bytes 4194304 | tf_op jit(solution)/shard_map/all_to_all | solution.py:176
  248.9 5.1 %fusion.135 = bf16[8,64,512]{2,1,0:T(8,128)(2,1)S(1)} fusion(bf16[512,8,64]{0,2,1:T(8,128)(2,1)S(1)} %bitcast.379, f32[8,512,512]{1,2,0:T(8,128)} %copy-done.2, f32[8,512]{1,0:T(8,128)S(1)} %log_add_fusion), kind=kOutput, calls=%fused_computation.217 | convolution fusion | flops 274989056 | bytes 9453568 | tf_op jit(solution)/shard_map/hqk,qhe->khe/dot_general | solution.py:328
  254.0 4.7 %multiply_reduce_fusion = (f32[8,512]{1,0:T(8,128)S(1)}, f32[8,512,512]{1,2,0:T(8,128)S(1)}) fusion(f32[8,512,512]{1,2,0:T(8,128)} %copy-done.2, f32[8,512]{1,0:T(8,128)S(1)} %log_add_fusion, bf16[512,8,64]{0,2,1:T(8,128)(2,1)S(1)} %bitcast.380, bf16[512,8,64]{0,2,1:T(8,128)(2,1)S(1)} %bitcast.382), kind=kOutput, calls=%fused_computation.9 | convolution fusion | flops 276819968 | bytes 17858560 | tf_op jit(solution)/shard_map/qhe,khe->hqk/dot_general | solution.py:315
  258.8 2.8 multiply_convert_fusion
  277.2 3.5 fusion.13
  281.1 12.9 %collective-permute-done.30 = bf16[2,64,1312]{2,1,0:T(8,128)(2,1)S(1)} collective-permute-done((bf16[2,64,1312]{2,1,0:T(8,128)(2,1)S(1)}, bf16[2,64,1312]{2,1,0:T(8,128)(2,1)S(1)}, u32[]{:S(2)}, u32[]{:S(2)}) %collective-permute-start.30) | collective-permute-done | bytes 335904 | tf_op jit(solution)/shard_map/ppermute | solution.py:102
  294.3 7.4 %collective-permute-done.28 = bf16[2,64,1312]{2,1,0:T(8,128)(2,1)S(1)} collective-permute-done((bf16[2,64,1312]{2,1,0:T(8,128)(2,1)S(1)}, bf16[2,64,1312]{2,1,0:T(8,128)(2,1)S(1)}, u32[]{:S(2)}, u32[]{:S(2)}) %collective-permute-start.28) | collective-permute-done | bytes 335904 | tf_op jit(solution)/shard_map/ppermute | solution.py:102
  301.7 5.7 %collective-permute-start.31 = (bf16[64,1312]{1,0:T(8,128)(2,1)S(1)}, bf16[64,1312]{1,0:T(8,128)(2,1)S(1)}, u32[]{:S(2)}, u32[]{:S(2)}) collective-permute-start(bf16[64,1312]{1,0:T(8,128)(2,1)S(1)} %fusion.177), channel_id=1, source_target_pairs={{0,16},{2,18},{4,20},{6,22},{8,24},{10,26},{12,28},{14,30},{16,0},... | collective-permute-start | bytes 503816 | tf_op jit(solution)/shard_map/ppermute | solution.py:102
  307.6 5.1 %collective-permute-done.26 = bf16[2,64,1312]{2,1,0:T(8,128)(2,1)S(1)} collective-permute-done((bf16[2,64,1312]{2,1,0:T(8,128)(2,1)S(1)}, bf16[2,64,1312]{2,1,0:T(8,128)(2,1)S(1)}, u32[]{:S(2)}, u32[]{:S(2)}) %collective-permute-start.26) | collective-permute-done | bytes 335904 | tf_op jit(solution)/shard_map/ppermute | solution.py:102
  312.7 4.9 %collective-permute-start.29 = (bf16[64,1312]{1,0:T(8,128)(2,1)S(1)}, bf16[64,1312]{1,0:T(8,128)(2,1)S(1)}, u32[]{:S(2)}, u32[]{:S(2)}) collective-permute-start(bf16[64,1312]{1,0:T(8,128)(2,1)S(1)} %fusion.176), channel_id=1, source_target_pairs={{0,16},{2,18},{4,20},{6,22},{8,24},{10,26},{12,28},{14,30},{16,0},... | collective-permute-start | bytes 503816 | tf_op jit(solution)/shard_map/ppermute | solution.py:102
  317.7 11.5 %collective-permute-done.29 = bf16[64,1312]{1,0:T(8,128)(2,1)S(1)} collective-permute-done((bf16[64,1312]{1,0:T(8,128)(2,1)S(1)}, bf16[64,1312]{1,0:T(8,128)(2,1)S(1)}, u32[]{:S(2)}, u32[]{:S(2)}) %collective-permute-start.29) | collective-permute-done | bytes 167968 | tf_op jit(solution)/shard_map/ppermute | solution.py:102
  333.2 4.6 %collective-permute-done.23 = bf16[2,2,64,512]{3,2,0,1:T(8,128)(2,1)S(1)} collective-permute-done((bf16[2,2,64,512]{3,2,0,1:T(8,128)(2,1)S(1)}, bf16[2,2,64,512]{3,2,0,1:T(8,128)(2,1)S(1)}, u32[]{:S(2)}, u32[]{:S(2)}) %collective-permute-start.23) | collective-permute-done | bytes 262176 | tf_op jit(solution)/shard_map/ppermute | solution.py:102
  338.0 5.6 %collective-permute-done.24 = bf16[2,64,512]{2,1,0:T(8,128)(2,1)S(1)} collective-permute-done((bf16[2,64,512]{2,1,0:T(8,128)(2,1)S(1)}, bf16[2,64,512]{2,1,0:T(8,128)(2,1)S(1)}, u32[]{:S(2)}, u32[]{:S(2)}) %collective-permute-start.24) | collective-permute-done | bytes 131104 | tf_op jit(solution)/shard_map/ppermute | solution.py:102
  344.4 3.8 fusion.86
  348.3 4.5 %select_convert_fusion.1 = (bf16[512,1024]{1,0:T(8,128)(2,1)S(1)}, bf16[512,1024]{1,0:T(8,128)(2,1)S(1)}, bf16[512,1024]{1,0:T(8,128)(2,1)S(1)}) fusion(pred[512]{0:T(512)(128)(4,1)S(1)} %iota_compare_fusion.6, f32[512,1024]{1,0:T(8,128)} %get-tuple-element.102, f32[512]{0:T(512)S(1)} %broadcast_multiply_fusion.12, f32[512]{0:T(512)S(1)} %copy-done.72, ...), kind=kLoop, calls=%fused_computation.151 | loop fusion | flops 14155776 | bytes 13652480 | tf_op jit(solution)/shard_map/convert.2
  355.4 4.7 %all-to-all-start.3 = ((bf16[16,64,1024]{2,1,0:T(8,128)(2,1)}), bf16[16,64,1024]{2,1,0:T(8,128)(2,1)}, u32[]{:S(2)}, u32[]{:S(2)}) async-start(bf16[16,64,1024]{2,1,0:T(8,128)(2,1)} %bitcast.79), calls=%async_computation.3 | async-start | bytes 4194304 | tf_op jit(solution)/shard_map/all_to_all | solution.py:176
  363.4 2.8 bitcast_add_fusion
  366.3 6.1 %collective-permute-done.17 = f32[2,2,1,2,64]{4,3,1,0,2:T(2,128)S(1)} collective-permute-done((f32[2,2,1,2,64]{4,3,1,0,2:T(2,128)S(1)}, f32[2,2,1,2,64]{4,3,1,0,2:T(2,128)S(1)}, u32[]{:S(2)}, u32[]{:S(2)}) %collective-permute-start.17) | collective-permute-done | bytes 2080 | tf_op jit(solution)/shard_map/ppermute | solution.py:102
  373.5 21.2 %collective-permute-done.18 = f32[2,1,2,64]{3,2,1,0:T(2,128)S(1)} collective-permute-done((f32[2,1,2,64]{3,2,1,0:T(2,128)S(1)}, f32[2,1,2,64]{3,2,1,0:T(2,128)S(1)}, u32[]{:S(2)}, u32[]{:S(2)}) %collective-permute-start.18) | collective-permute-done | bytes 1056 | tf_op jit(solution)/shard_map/ppermute | solution.py:102
  394.8 4.4 %collective-permute-start.19 = (f32[1,2,64]{2,1,0:T(2,128)S(1)}, f32[1,2,64]{2,1,0:T(2,128)S(1)}, u32[]{:S(2)}, u32[]{:S(2)}) collective-permute-start(f32[1,2,64]{2,1,0:T(2,128)S(1)} %fusion.194), channel_id=1, source_target_pairs={{0,16},{2,18},{4,20},{6,22},{8,24},{10,26},{12,28},{14,30},{16,0},... | collective-permute-start | bytes 1544 | tf_op jit(solution)/shard_map/ppermute | solution.py:102
  399.8 9.0 %collective-permute-done.19 = f32[1,2,64]{2,1,0:T(2,128)S(1)} collective-permute-done((f32[1,2,64]{2,1,0:T(2,128)S(1)}, f32[1,2,64]{2,1,0:T(2,128)S(1)}, u32[]{:S(2)}, u32[]{:S(2)}) %collective-permute-start.19) | collective-permute-done | bytes 544 | tf_op jit(solution)/shard_map/ppermute | solution.py:102
  415.2 3.7 gather_fusion.7
  418.9 4.2 bitcast_convert_fusion
  424.8 9.7 %collective-permute-done.22 = bf16[64,1536]{1,0:T(8,128)(2,1)S(1)} collective-permute-done((bf16[64,1536]{1,0:T(8,128)(2,1)S(1)}, bf16[64,1536]{1,0:T(8,128)(2,1)S(1)}, u32[]{:S(2)}, u32[]{:S(2)}) %collective-permute-start.22) | collective-permute-done | bytes 196640 | tf_op jit(solution)/shard_map/ppermute | solution.py:102
  (436 shorter events, 140.6 us)
Async XLA Ops:
  0.6 126.3 %copy-start = (bf16[1312,1024]{1,0:T(8,128)(2,1)S(1)}, bf16[1312,1024]{1,0:T(8,128)(2,1)}, u32[]{:S(2)}) copy-start(bf16[1312,1024]{1,0:T(8,128)(2,1)} %param.18) | copy-start | bytes 8060932
  6.2 48.6 %all-to-all-start = ((bf16[16,64,1024]{2,1,0:T(8,128)(2,1)}), bf16[16,64,1024]{2,1,0:T(8,128)(2,1)}, u32[]{:S(2)}, u32[]{:S(2)}) async-start(bf16[16,64,1024]{2,1,0:T(8,128)(2,1)} %bitcast.358), calls=%async_computation | async-start | bytes 4194304 | tf_op jit(solution)/shard_map/all_to_all | solution.py:176
  54.9 52.3 %all-to-all-start.1 = ((bf16[16,64,1024]{2,1,0:T(8,128)(2,1)}), bf16[16,64,1024]{2,1,0:T(8,128)(2,1)}, u32[]{:S(2)}, u32[]{:S(2)}) async-start(bf16[16,64,1024]{2,1,0:T(8,128)(2,1)} %bitcast.357), calls=%async_computation.1 | async-start | bytes 4194304 | tf_op jit(solution)/shard_map/all_to_all | solution.py:176
  94.2 26.3 %collective-permute-start = (bf16[512,1024]{1,0:T(8,128)(2,1)}, bf16[512,1024]{1,0:T(8,128)(2,1)}, u32[]{:S(2)}, u32[]{:S(2)}) collective-permute-start(bf16[512,1024]{1,0:T(8,128)(2,1)} %convolution_convert_fusion.3), channel_id=1, source_target_pairs={{0,1},{1,0},{2,3},{3,2},{4,5},{5,4},{6,7},{7,6},{8,9},{9,8},{10,11... | collective-permute-start | bytes 3145736 | tf_op jit(solution)/shard_map/ppermute | solution.py:72
  105.9 37.2 %collective-permute-start.1 = (bf16[512,1024]{1,0:T(8,128)(2,1)}, bf16[512,1024]{1,0:T(8,128)(2,1)}, u32[]{:S(2)}, u32[]{:S(2)}) collective-permute-start(bf16[512,1024]{1,0:T(8,128)(2,1)} %convolution_convert_fusion.2), channel_id=1, source_target_pairs={{0,1},{1,0},{2,3},{3,2},{4,5},{5,4},{6,7},{7,6},{8,9},{9,8},{10,11... | collective-permute-start | bytes 3145736 | tf_op jit(solution)/shard_map/ppermute | solution.py:72
  112.9 36.2 %copy-start.13 = (bf16[512,1024]{1,0:T(8,128)(2,1)}, bf16[512,1024]{1,0:T(8,128)(2,1)S(1)}, u32[]{:S(2)}) copy-start(bf16[512,1024]{1,0:T(8,128)(2,1)S(1)} %get-tuple-element.130) | copy-start | bytes 3145732
  122.8 58.2 %copy-start.4 = (f32[512,1024]{1,0:T(8,128)}, f32[512,1024]{1,0:T(8,128)S(1)}, u32[]{:S(2)}) copy-start(f32[512,1024]{1,0:T(8,128)S(1)} %get-tuple-element.108) | copy-start | bytes 6291460
  133.6 45.9 %collective-permute-start.2 = (bf16[512,1024]{1,0:T(8,128)(2,1)S(1)}, bf16[512,1024]{1,0:T(8,128)(2,1)S(1)}, u32[]{:S(2)}, u32[]{:S(2)}) collective-permute-start(bf16[512,1024]{1,0:T(8,128)(2,1)S(1)} %add_convert_fusion.1), channel_id=1, source_target_pairs={{0,1},{1,0},{2,3},{3,2},{4,5},{5,4},{6,7},{7,6},{8,9},{9,8},{10,11... | collective-permute-start | bytes 3145736 | tf_op jit(solution)/shard_map/ppermute | solution.py:72
  145.1 62.8 %copy-start.6 = (f32[512,1024]{1,0:T(8,128)}, f32[512,1024]{1,0:T(8,128)S(1)}, u32[]{:S(2)}) copy-start(f32[512,1024]{1,0:T(8,128)S(1)} %get-tuple-element.106) | copy-start | bytes 6291460
  156.0 51.9 %copy-start.31 = (bf16[512,1024]{1,0:T(8,128)(2,1)}, bf16[512,1024]{1,0:T(8,128)(2,1)S(1)}, u32[]{:S(2)}) copy-start(bf16[512,1024]{1,0:T(8,128)(2,1)S(1)} %add_convert_fusion) | copy-start | bytes 3145732
  156.1 49.8 %collective-permute-start.6 = (bf16[512,1024]{1,0:T(8,128)(2,1)S(1)}, bf16[512,1024]{1,0:T(8,128)(2,1)S(1)}, u32[]{:S(2)}, u32[]{:S(2)}) collective-permute-start(bf16[512,1024]{1,0:T(8,128)(2,1)S(1)} %add_convert_fusion), channel_id=1, source_target_pairs={{0,1},{1,0},{2,3},{3,2},{4,5},{5,4},{6,7},{7,6},{8,9},{9,8},{10,11... | collective-permute-start | bytes 3145736 | tf_op jit(solution)/shard_map/ppermute | solution.py:72
  167.9 29.8 %collective-permute-start.9 = (bf16[2,2,2,64,1312]{4,3,2,1,0:T(8,128)(2,1)}, bf16[2,2,2,64,1312]{4,3,2,1,0:T(8,128)(2,1)}, u32[]{:S(2)}, u32[]{:S(2)}) collective-permute-start(bf16[2,2,2,64,1312]{4,3,2,1,0:T(8,128)(2,1)} %fusion.129), channel_id=1, source_target_pairs={{0,2},{2,0},{4,6},{6,4},{8,10},{10,8},{12,14},{14,12},{16,18},{18,... | collective-permute-start | bytes 4030472 | tf_op jit(solution)/shard_map/ppermute | solution.py:102
  167.9 33.1 %collective-permute-start.8 = (bf16[2,2,2,64,1312]{4,3,2,1,0:T(8,128)(2,1)}, bf16[2,2,2,64,1312]{4,3,2,1,0:T(8,128)(2,1)}, u32[]{:S(2)}, u32[]{:S(2)}) collective-permute-start(bf16[2,2,2,64,1312]{4,3,2,1,0:T(8,128)(2,1)} %fusion.128), channel_id=1, source_target_pairs={{0,2},{2,0},{4,6},{6,4},{8,10},{10,8},{12,14},{14,12},{16,18},{18,... | collective-permute-start | bytes 4030472 | tf_op jit(solution)/shard_map/ppermute | solution.py:102
  173.8 33.9 %collective-permute-start.7 = (bf16[2,2,2,64,1312]{4,3,2,1,0:T(8,128)(2,1)}, bf16[2,2,2,64,1312]{4,3,2,1,0:T(8,128)(2,1)}, u32[]{:S(2)}, u32[]{:S(2)}) collective-permute-start(bf16[2,2,2,64,1312]{4,3,2,1,0:T(8,128)(2,1)} %fusion.127), channel_id=1, source_target_pairs={{0,2},{2,0},{4,6},{6,4},{8,10},{10,8},{12,14},{14,12},{16,18},{18,... | collective-permute-start | bytes 4030472 | tf_op jit(solution)/shard_map/ppermute | solution.py:102
  179.5 34.8 %collective-permute-start.4 = (bf16[512,1024]{1,0:T(8,128)(2,1)}, bf16[512,1024]{1,0:T(8,128)(2,1)}, u32[]{:S(2)}, u32[]{:S(2)}) collective-permute-start(bf16[512,1024]{1,0:T(8,128)(2,1)} %convolution_convert_fusion), channel_id=1, source_target_pairs={{0,1},{1,0},{2,3},{3,2},{4,5},{5,4},{6,7},{7,6},{8,9},{9,8},{10,11... | collective-permute-start | bytes 3145736 | tf_op jit(solution)/shard_map/ppermute | solution.py:72
  197.7 35.2 %collective-permute-start.3 = (bf16[512,1024]{1,0:T(8,128)(2,1)}, bf16[512,1024]{1,0:T(8,128)(2,1)}, u32[]{:S(2)}, u32[]{:S(2)}) collective-permute-start(bf16[512,1024]{1,0:T(8,128)(2,1)} %convolution_convert_fusion.1), channel_id=1, source_target_pairs={{0,1},{1,0},{2,3},{3,2},{4,5},{5,4},{6,7},{7,6},{8,9},{9,8},{10,11... | collective-permute-start | bytes 3145736 | tf_op jit(solution)/shard_map/ppermute | solution.py:72
  201.0 79.9 %collective-permute-start.5 = (bf16[512,1024]{1,0:T(8,128)(2,1)}, bf16[512,1024]{1,0:T(8,128)(2,1)}, u32[]{:S(2)}, u32[]{:S(2)}) collective-permute-start(bf16[512,1024]{1,0:T(8,128)(2,1)} %fusion.124), channel_id=1, source_target_pairs={{0,1},{1,0},{2,3},{3,2},{4,5},{5,4},{6,7},{7,6},{8,9},{9,8},{10,11... | collective-permute-start | bytes 3145736 | tf_op jit(solution)/shard_map/ppermute | solution.py:72
  205.9 65.6 %collective-permute-start.13 = (bf16[2,2,64,1312]{3,2,1,0:T(8,128)(2,1)}, bf16[2,2,64,1312]{3,2,1,0:T(8,128)(2,1)}, u32[]{:S(2)}, u32[]{:S(2)}) collective-permute-start(bf16[2,2,64,1312]{3,2,1,0:T(8,128)(2,1)} %fusion.164), channel_id=1, source_target_pairs={{0,4},{2,6},{4,0},{6,2},{8,12},{10,14},{12,8},{14,10},{16,20},{18,... | collective-permute-start | bytes 2015240 | tf_op jit(solution)/shard_map/ppermute | solution.py:102
  207.7 65.2 %collective-permute-start.12 = (bf16[2,2,64,1312]{3,2,1,0:T(8,128)(2,1)}, bf16[2,2,64,1312]{3,2,1,0:T(8,128)(2,1)}, u32[]{:S(2)}, u32[]{:S(2)}) collective-permute-start(bf16[2,2,64,1312]{3,2,1,0:T(8,128)(2,1)} %fusion.163), channel_id=1, source_target_pairs={{0,4},{2,6},{4,0},{6,2},{8,12},{10,14},{12,8},{14,10},{16,20},{18,... | collective-permute-start | bytes 2015240 | tf_op jit(solution)/shard_map/ppermute | solution.py:102
  209.0 23.9 %copy-start.5 = (f32[512,1024]{1,0:T(8,128)S(1)}, f32[512,1024]{1,0:T(8,128)}, u32[]{:S(2)}) copy-start(f32[512,1024]{1,0:T(8,128)} %copy-done.4) | copy-start | bytes 6291460
  209.0 23.9 %copy-start.7 = (f32[512,1024]{1,0:T(8,128)S(1)}, f32[512,1024]{1,0:T(8,128)}, u32[]{:S(2)}) copy-start(f32[512,1024]{1,0:T(8,128)} %copy-done.6) | copy-start | bytes 6291460
  209.0 23.9 %copy-start.32 = (bf16[512,1024]{1,0:T(8,128)(2,1)S(1)}, bf16[512,1024]{1,0:T(8,128)(2,1)}, u32[]{:S(2)}) copy-start(bf16[512,1024]{1,0:T(8,128)(2,1)} %copy-done.31) | copy-start | bytes 3145732
  209.0 23.9 %copy-start.34 = (bf16[512,1024]{1,0:T(8,128)(2,1)S(1)}, bf16[512,1024]{1,0:T(8,128)(2,1)}, u32[]{:S(2)}) copy-start(bf16[512,1024]{1,0:T(8,128)(2,1)} %copy-done.33) | copy-start | bytes 3145732
  214.3 54.3 %collective-permute-start.11 = (bf16[2,2,64,1312]{3,2,1,0:T(8,128)(2,1)}, bf16[2,2,64,1312]{3,2,1,0:T(8,128)(2,1)}, u32[]{:S(2)}, u32[]{:S(2)}) collective-permute-start(bf16[2,2,64,1312]{3,2,1,0:T(8,128)(2,1)} %fusion.162), channel_id=1, source_target_pairs={{0,4},{2,6},{4,0},{6,2},{8,12},{10,14},{12,8},{14,10},{16,20},{18,... | collective-permute-start | bytes 2015240 | tf_op jit(solution)/shard_map/ppermute | solution.py:102
  240.4 89.6 %collective-permute-start.14 = (bf16[2,2,2,64,512]{4,3,0,1,2:T(8,128)(2,1)}, bf16[2,2,2,64,512]{4,3,0,1,2:T(8,128)(2,1)}, u32[]{:S(2)}, u32[]{:S(2)}) collective-permute-start(bf16[2,2,2,64,512]{4,3,0,1,2:T(8,128)(2,1)} %fusion.165), channel_id=1, source_target_pairs={{0,2},{2,0},{4,6},{6,4},{8,10},{10,8},{12,14},{14,12},{16,18},{18,... | collective-permute-start | bytes 1572872 | tf_op jit(solution)/shard_map/ppermute | solution.py:102
  242.8 112.6 %all-to-all-start.2 = ((bf16[16,64,1024]{2,1,0:T(8,128)(2,1)}), bf16[16,64,1024]{2,1,0:T(8,128)(2,1)}, u32[]{:S(2)}, u32[]{:S(2)}) async-start(bf16[16,64,1024]{2,1,0:T(8,128)(2,1)} %bitcast.40), calls=%async_computation.2 | async-start | bytes 4194304 | tf_op jit(solution)/shard_map/all_to_all | solution.py:176
  268.6 75.8 %copy-start.29 = (bf16[512,1024]{1,0:T(8,128)(2,1)}, bf16[512,1024]{1,0:T(8,128)(2,1)S(1)}, u32[]{:S(2)}) copy-start(bf16[512,1024]{1,0:T(8,128)(2,1)S(1)} %fusion.121) | copy-start | bytes 3145732
  268.6 75.4 %collective-permute-start.10 = (bf16[512,1024]{1,0:T(8,128)(2,1)S(1)}, bf16[512,1024]{1,0:T(8,128)(2,1)S(1)}, u32[]{:S(2)}, u32[]{:S(2)}) collective-permute-start(bf16[512,1024]{1,0:T(8,128)(2,1)S(1)} %fusion.121), channel_id=1, source_target_pairs={{0,1},{1,0},{2,3},{3,2},{4,5},{5,4},{6,7},{7,6},{8,9},{9,8},{10,11... | collective-permute-start | bytes 3145736 | tf_op jit(solution)/shard_map/ppermute | solution.py:72
  275.1 18.9 %collective-permute-start.30 = (bf16[2,64,1312]{2,1,0:T(8,128)(2,1)S(1)}, bf16[2,64,1312]{2,1,0:T(8,128)(2,1)S(1)}, u32[]{:S(2)}, u32[]{:S(2)}) collective-permute-start(bf16[2,64,1312]{2,1,0:T(8,128)(2,1)S(1)} %fusion.169), channel_id=1, source_target_pairs={{0,8},{2,10},{4,12},{6,14},{8,0},{10,2},{12,4},{14,6},{16,24},{18,... | collective-permute-start | bytes 1007624 | tf_op jit(solution)/shard_map/ppermute | solution.py:102
  277.1 24.6 %collective-permute-start.28 = (bf16[2,64,1312]{2,1,0:T(8,128)(2,1)S(1)}, bf16[2,64,1312]{2,1,0:T(8,128)(2,1)S(1)}, u32[]{:S(2)}, u32[]{:S(2)}) collective-permute-start(bf16[2,64,1312]{2,1,0:T(8,128)(2,1)S(1)} %fusion.168), channel_id=1, source_target_pairs={{0,8},{2,10},{4,12},{6,14},{8,0},{10,2},{12,4},{14,6},{16,24},{18,... | collective-permute-start | bytes 1007624 | tf_op jit(solution)/shard_map/ppermute | solution.py:102
  280.7 50.5 %copy-start.35 = (f32[1024,1536]{1,0:T(8,128)}, f32[1024,1536]{1,0:T(8,128)S(1)}, u32[]{:S(2)}) copy-start(f32[1024,1536]{1,0:T(8,128)S(1)} %fusion.13) | copy-start | bytes 18874372
  280.9 63.4 %collective-permute-start.15 = (bf16[2,2,2,64,1536]{4,3,0,1,2:T(8,128)(2,1)S(1)}, bf16[2,2,2,64,1536]{4,3,0,1,2:T(8,128)(2,1)}, u32[]{:S(2)}, u32[]{:S(2)}) collective-permute-start(bf16[2,2,2,64,1536]{4,3,0,1,2:T(8,128)(2,1)S(1)} %fusion.104), channel_id=1, source_target_pairs={{0,2},{2,0},{4,6},{6,4},{8,10},{10,8},{12,14},{14,12},{16,18},{18,... | collective-permute-start | bytes 4718600 | tf_op jit(solution)/shard_map/ppermute | solution.py:102
  294.0 18.7 %collective-permute-start.26 = (bf16[2,64,1312]{2,1,0:T(8,128)(2,1)S(1)}, bf16[2,64,1312]{2,1,0:T(8,128)(2,1)S(1)}, u32[]{:S(2)}, u32[]{:S(2)}) collective-permute-start(bf16[2,64,1312]{2,1,0:T(8,128)(2,1)S(1)} %fusion.167), channel_id=1, source_target_pairs={{0,8},{2,10},{4,12},{6,14},{8,0},{10,2},{12,4},{14,6},{16,24},{18,... | collective-permute-start | bytes 1007624 | tf_op jit(solution)/shard_map/ppermute | solution.py:102
  301.7 15.9 %collective-permute-start.31 = (bf16[64,1312]{1,0:T(8,128)(2,1)S(1)}, bf16[64,1312]{1,0:T(8,128)(2,1)S(1)}, u32[]{:S(2)}, u32[]{:S(2)}) collective-permute-start(bf16[64,1312]{1,0:T(8,128)(2,1)S(1)} %fusion.177), channel_id=1, source_target_pairs={{0,16},{2,18},{4,20},{6,22},{8,24},{10,26},{12,28},{14,30},{16,0},... | collective-permute-start | bytes 503816 | tf_op jit(solution)/shard_map/ppermute | solution.py:102
  312.7 16.5 %collective-permute-start.29 = (bf16[64,1312]{1,0:T(8,128)(2,1)S(1)}, bf16[64,1312]{1,0:T(8,128)(2,1)S(1)}, u32[]{:S(2)}, u32[]{:S(2)}) collective-permute-start(bf16[64,1312]{1,0:T(8,128)(2,1)S(1)} %fusion.176), channel_id=1, source_target_pairs={{0,16},{2,18},{4,20},{6,22},{8,24},{10,26},{12,28},{14,30},{16,0},... | collective-permute-start | bytes 503816 | tf_op jit(solution)/shard_map/ppermute | solution.py:102
  317.6 15.5 %collective-permute-start.27 = (bf16[64,1312]{1,0:T(8,128)(2,1)S(1)}, bf16[64,1312]{1,0:T(8,128)(2,1)S(1)}, u32[]{:S(2)}, u32[]{:S(2)}) collective-permute-start(bf16[64,1312]{1,0:T(8,128)(2,1)S(1)} %fusion.175), channel_id=1, source_target_pairs={{0,16},{2,18},{4,20},{6,22},{8,24},{10,26},{12,28},{14,30},{16,0},... | collective-permute-start | bytes 503816 | tf_op jit(solution)/shard_map/ppermute | solution.py:102
  331.3 6.4 %collective-permute-start.23 = (bf16[2,2,64,512]{3,2,0,1:T(8,128)(2,1)S(1)}, bf16[2,2,64,512]{3,2,0,1:T(8,128)(2,1)S(1)}, u32[]{:S(2)}, u32[]{:S(2)}) collective-permute-start(bf16[2,2,64,512]{3,2,0,1:T(8,128)(2,1)S(1)} %fusion.173), channel_id=1, source_target_pairs={{0,4},{2,6},{4,0},{6,2},{8,12},{10,14},{12,8},{14,10},{16,20},{18,... | collective-permute-start | bytes 786440 | tf_op jit(solution)/shard_map/ppermute | solution.py:102
  337.9 5.7 %collective-permute-start.24 = (bf16[2,64,512]{2,1,0:T(8,128)(2,1)S(1)}, bf16[2,64,512]{2,1,0:T(8,128)(2,1)S(1)}, u32[]{:S(2)}, u32[]{:S(2)}) collective-permute-start(bf16[2,64,512]{2,1,0:T(8,128)(2,1)S(1)} %fusion.178), channel_id=1, source_target_pairs={{0,8},{2,10},{4,12},{6,14},{8,0},{10,2},{12,4},{14,6},{16,24},{18,... | collective-permute-start | bytes 393224 | tf_op jit(solution)/shard_map/ppermute | solution.py:102
  343.7 18.0 %collective-permute-start.25 = (bf16[64,512]{1,0:T(8,128)(2,1)S(1)}, bf16[64,512]{1,0:T(8,128)(2,1)S(1)}, u32[]{:S(2)}, u32[]{:S(2)}) collective-permute-start(bf16[64,512]{1,0:T(8,128)(2,1)S(1)} %fusion.180), channel_id=1, source_target_pairs={{0,16},{2,18},{4,20},{6,22},{8,24},{10,26},{12,28},{14,30},{16,0},... | collective-permute-start | bytes 196616 | tf_op jit(solution)/shard_map/ppermute | solution.py:102
  355.4 59.8 %all-to-all-start.3 = ((bf16[16,64,1024]{2,1,0:T(8,128)(2,1)}), bf16[16,64,1024]{2,1,0:T(8,128)(2,1)}, u32[]{:S(2)}, u32[]{:S(2)}) async-start(bf16[16,64,1024]{2,1,0:T(8,128)(2,1)} %bitcast.79), calls=%async_computation.3 | async-start | bytes 4194304 | tf_op jit(solution)/shard_map/all_to_all | solution.py:176
  360.1 1.6 collective-permute-start.16
  361.7 37.4 %copy-start.55 = (f32[2,64,512]{2,1,0:T(8,128)S(1)}, f32[2,64,512]{2,1,0:T(8,128)}, u32[]{:S(2)}) copy-start(f32[2,64,512]{2,1,0:T(8,128)} %copy-done.54) | copy-start | bytes 786436
  361.7 10.6 %collective-permute-start.17 = (f32[2,2,1,2,64]{4,3,1,0,2:T(2,128)S(1)}, f32[2,2,1,2,64]{4,3,1,0,2:T(2,128)S(1)}, u32[]{:S(2)}, u32[]{:S(2)}) collective-permute-start(f32[2,2,1,2,64]{4,3,1,0,2:T(2,128)S(1)} %fusion.188), channel_id=1, source_target_pairs={{0,4},{2,6},{4,0},{6,2},{8,12},{10,14},{12,8},{14,10},{16,20},{18,... | collective-permute-start | bytes 6152 | tf_op jit(solution)/shard_map/ppermute | solution.py:102
  372.3 22.4 %collective-permute-start.18 = (f32[2,1,2,64]{3,2,1,0:T(2,128)S(1)}, f32[2,1,2,64]{3,2,1,0:T(2,128)S(1)}, u32[]{:S(2)}, u32[]{:S(2)}) collective-permute-start(f32[2,1,2,64]{3,2,1,0:T(2,128)S(1)} %fusion.191), channel_id=1, source_target_pairs={{0,8},{2,10},{4,12},{6,14},{8,0},{10,2},{12,4},{14,6},{16,24},{18,... | collective-permute-start | bytes 3080 | tf_op jit(solution)/shard_map/ppermute | solution.py:102
  372.9 36.0 %collective-permute-start.20 = (bf16[2,2,64,1536]{3,2,0,1:T(8,128)(2,1)S(1)}, bf16[2,2,64,1536]{3,2,0,1:T(8,128)(2,1)S(1)}, u32[]{:S(2)}, u32[]{:S(2)}) collective-permute-start(bf16[2,2,64,1536]{3,2,0,1:T(8,128)(2,1)S(1)} %fusion.161), channel_id=1, source_target_pairs={{0,4},{2,6},{4,0},{6,2},{8,12},{10,14},{12,8},{14,10},{16,20},{18,... | collective-permute-start | bytes 2359304 | tf_op jit(solution)/shard_map/ppermute | solution.py:102
  394.8 14.0 %collective-permute-start.19 = (f32[1,2,64]{2,1,0:T(2,128)S(1)}, f32[1,2,64]{2,1,0:T(2,128)S(1)}, u32[]{:S(2)}, u32[]{:S(2)}) collective-permute-start(f32[1,2,64]{2,1,0:T(2,128)S(1)} %fusion.194), channel_id=1, source_target_pairs={{0,16},{2,18},{4,20},{6,22},{8,24},{10,26},{12,28},{14,30},{16,0},... | collective-permute-start | bytes 1544 | tf_op jit(solution)/shard_map/ppermute | solution.py:102
  409.1 14.0 %collective-permute-start.21 = (bf16[2,64,1536]{2,1,0:T(8,128)(2,1)S(1)}, bf16[2,64,1536]{2,1,0:T(8,128)(2,1)S(1)}, u32[]{:S(2)}, u32[]{:S(2)}) collective-permute-start(bf16[2,64,1536]{2,1,0:T(8,128)(2,1)S(1)} %fusion.166), channel_id=1, source_target_pairs={{0,8},{2,10},{4,12},{6,14},{8,0},{10,2},{12,4},{14,6},{16,24},{18,... | collective-permute-start | bytes 1179656 | tf_op jit(solution)/shard_map/ppermute | solution.py:102
  423.3 11.2 %collective-permute-start.22 = (bf16[64,1536]{1,0:T(8,128)(2,1)S(1)}, bf16[64,1536]{1,0:T(8,128)(2,1)S(1)}, u32[]{:S(2)}, u32[]{:S(2)}) collective-permute-start(bf16[64,1536]{1,0:T(8,128)(2,1)S(1)} %fusion.174), channel_id=1, source_target_pairs={{0,16},{2,18},{4,20},{6,22},{8,24},{10,26},{12,28},{14,30},{16,0},... | collective-permute-start | bytes 589832 | tf_op jit(solution)/shard_map/ppermute | solution.py:102
  (88 other events, 505.9 us)
